TPU v7x, 32 devices: a whole 2x2x4 slice. The times are simulated.
32 devices in a mesh: dp: 8 (over z, y), sp: 4 (over x, core).
Axes of the slice: x: 2, y: 2, z: 4, core: 2. Of those that a mesh axis runs over, the one named last changes fastest.
Arguments:
- tokens: bfloat16 [32, 96, 48, 256], P('dp', 'sp')
- grad_out: bfloat16 [32, 48, 24, 512], P(('dp', 'sp'))
- rel_index: int32 [144, 144], replicated
- norm_merge: bfloat16 [2, 1024], replicated
- w_reduce: bfloat16 [1024, 512], replicated
- norm_attn: bfloat16 [2, 512], replicated
- w_qkv: bfloat16 [512, 1536], replicated
- b_qkv: bfloat16 [1536], replicated
- rel_table: bfloat16 [529, 16], replicated
- w_proj: bfloat16 [512, 512], replicated
- b_proj: bfloat16 [512], replicated
- norm_mlp: bfloat16 [2, 512], replicated
- w_fc1: bfloat16 [512, 2048], replicated
- b_fc1: bfloat16 [2048], replicated
- w_fc2: bfloat16 [2048, 512], replicated
- b_fc2: bfloat16 [512], replicated
Outputs:
- output 1: bfloat16 [32, 48, 24, 512], P(('dp', 'sp'))
- output 2: bfloat16 [32, 96, 48, 256], P('dp', 'sp')
- output 3: float32 [2, 1024], replicated
- output 4: float32 [1024, 512], replicated
- output 5: float32 [2, 512], replicated
- output 6: float32 [512, 1536], replicated
- output 7: float32 [1536], replicated
- output 8: float32 [529, 16], replicated
- output 9: float32 [512, 512], replicated
- output 10: float32 [512], replicated
- output 11: float32 [2, 512], replicated
- output 12: float32 [512, 2048], replicated
- output 13: float32 [2048], replicated
- output 14: float32 [2048, 512], replicated
- output 15: float32 [512], replicated
All inputs are finite; a program needn't handle non-finite values.
Results may differ from a plain program's by a relative error of at most 0.02.
Values are sent between devices in bfloat16 or wider.
A program may use at most 1 GiB of HBM per device.

v0:
```python
import functools
import math
import jax
import jax.numpy as jnp
from jax import lax
from jax.sharding import PartitionSpec as P

NORM_EPS = 1e-5


def layer_norm(values, norm_gain, norm_shift, norm_axes):
    row_mean = jnp.mean(values, axis=norm_axes, keepdims=True)
    centred = values - row_mean
    row_var = jnp.mean(centred * centred, axis=norm_axes, keepdims=True)
    return centred * lax.rsqrt(row_var + NORM_EPS) * norm_gain + norm_shift


def block_norm(values, norm_pair):
    return layer_norm(values, norm_pair[0], norm_pair[1], (-1,))


def merge_norm(tok_f32, norm_split):
    return layer_norm(tok_f32, norm_split[0], norm_split[1], (3, 6))


def merge_layout(norm_merge, w_reduce):
    in_chans = w_reduce.shape[0] // 4
    norm_split = norm_merge.reshape(2, 2, 2, in_chans).transpose(0, 2, 1, 3).reshape(2, 2, 1, 1, 2 * in_chans)
    w_split = w_reduce.reshape(2, 2, in_chans, -1).transpose(1, 0, 2, 3).reshape(2, 2 * in_chans, -1)
    return norm_split.astype(jnp.float32), w_split


def rows_per_step(total_rows, row_tokens):
    return max(count for count in range(1, total_rows + 1) if total_rows % count == 0 and count * row_tokens <= 1024) if row_tokens <= 1024 else 1


def block_step(tok_img, cot_img, rel_index, weights):
    (norm_merge, w_reduce, norm_attn, w_qkv, b_qkv, rel_table, w_proj, b_proj, norm_mlp, w_fc1, b_fc1, w_fc2, b_fc2) = weights
    n_img, height, img_width, in_chans = tok_img.shape
    model_dim = w_reduce.shape[1]
    n_heads = rel_table.shape[1]
    head_dim = model_dim // n_heads
    seq_len = rel_index.shape[0]
    window = math.isqrt(seq_len)
    win_rows = height // (2 * window)
    win_cols = img_width // (2 * window)
    q_scale = head_dim ** -0.5
    norm_split, w_split = merge_layout(norm_merge, w_reduce)
    tok_f32 = tok_img.reshape(n_img, win_rows, window, 2, win_cols, window, 2 * in_chans).astype(jnp.float32)
    merged_in = merge_norm(tok_f32, norm_split).astype(jnp.bfloat16)
    h_zero = jnp.einsum('naprctk,rkd->nacptd', merged_in, w_split, preferred_element_type=jnp.float32).astype(jnp.bfloat16).reshape(-1, seq_len, model_dim)
    pos_bias = jnp.take(rel_table, rel_index.reshape(-1), axis=0).astype(jnp.float32).T.reshape(n_heads, seq_len, seq_len)
    norm_one = norm_attn.astype(jnp.float32)
    h_zero_f = h_zero.astype(jnp.float32)
    normed_one = block_norm(h_zero_f, norm_one).astype(jnp.bfloat16)
    qkv_all = (jnp.einsum('nlc,ck->nlk', normed_one, w_qkv, preferred_element_type=jnp.float32) + b_qkv.astype(jnp.float32)).astype(jnp.bfloat16).reshape(-1, seq_len, 3, n_heads, head_dim)
    q_heads = qkv_all[:, :, 0]
    k_heads = qkv_all[:, :, 1]
    v_heads = qkv_all[:, :, 2]
    scores = jnp.einsum('nlhe,nmhe->nhlm', q_heads, k_heads, preferred_element_type=jnp.float32) * q_scale + pos_bias
    attn_prob = jax.nn.softmax(scores, axis=-1)
    prob_bf = attn_prob.astype(jnp.bfloat16)
    attn_out = jnp.einsum('nhlm,nmhe->nlhe', prob_bf, v_heads, preferred_element_type=jnp.float32).astype(jnp.bfloat16).reshape(-1, seq_len, model_dim)
    h_one = (h_zero_f + jnp.einsum('nlc,cd->nld', attn_out, w_proj, preferred_element_type=jnp.float32) + b_proj.astype(jnp.float32)).astype(jnp.bfloat16)
    h_one_f = h_one.astype(jnp.float32)
    norm_two = norm_mlp.astype(jnp.float32)
    normed_two = block_norm(h_one_f, norm_two).astype(jnp.bfloat16)
    pre_act = jnp.einsum('nlc,cf->nlf', normed_two, w_fc1, preferred_element_type=jnp.float32) + b_fc1.astype(jnp.float32)
    hidden = jax.nn.gelu(pre_act, approximate=False).astype(jnp.bfloat16)
    out_win = (h_one_f + jnp.einsum('nlf,fd->nld', hidden, w_fc2, preferred_element_type=jnp.float32) + b_fc2.astype(jnp.float32)).astype(jnp.bfloat16)
    result = out_win.reshape(n_img, win_rows, win_cols, window, window, model_dim).transpose(0, 1, 3, 2, 4, 5).reshape(n_img, win_rows * window, win_cols * window, model_dim)
    d_out = cot_img.reshape(n_img, win_rows, window, win_cols, window, model_dim).transpose(0, 1, 3, 2, 4, 5).reshape(-1, seq_len, model_dim)
    d_out_f = d_out.astype(jnp.float32)
    g_b_fc2 = jnp.sum(d_out_f, axis=(0, 1))
    g_w_fc2 = jnp.einsum('nlf,nld->fd', hidden, d_out, preferred_element_type=jnp.float32)
    d_hidden = jnp.einsum('nld,fd->nlf', d_out, w_fc2, preferred_element_type=jnp.float32)
    gelu_pull = jax.vjp(functools.partial(jax.nn.gelu, approximate=False), pre_act)[1]
    d_pre = gelu_pull(d_hidden)[0]
    d_pre_bf = d_pre.astype(jnp.bfloat16)
    g_b_fc1 = jnp.sum(d_pre, axis=(0, 1))
    g_w_fc1 = jnp.einsum('nlc,nlf->cf', normed_two, d_pre_bf, preferred_element_type=jnp.float32)
    d_normed_two = jnp.einsum('nlf,cf->nlc', d_pre_bf, w_fc1, preferred_element_type=jnp.float32)
    d_h_one_ln, g_norm_mlp = jax.vjp(block_norm, h_one_f, norm_two)[1](d_normed_two)
    d_h_one = d_out_f + d_h_one_ln
    d_h_one_bf = d_h_one.astype(jnp.bfloat16)
    g_b_proj = jnp.sum(d_h_one, axis=(0, 1))
    g_w_proj = jnp.einsum('nlc,nld->cd', attn_out, d_h_one_bf, preferred_element_type=jnp.float32)
    d_attn = jnp.einsum('nld,cd->nlc', d_h_one_bf, w_proj, preferred_element_type=jnp.float32).astype(jnp.bfloat16).reshape(-1, seq_len, n_heads, head_dim)
    d_prob = jnp.einsum('nlhe,nmhe->nhlm', d_attn, v_heads, preferred_element_type=jnp.float32)
    d_v_heads = jnp.einsum('nhlm,nlhe->nmhe', prob_bf, d_attn, preferred_element_type=jnp.float32)
    d_scores = attn_prob * (d_prob - jnp.sum(d_prob * attn_prob, axis=-1, keepdims=True))
    g_bias = jnp.sum(d_scores, axis=0)
    g_rel_table = jax.ops.segment_sum(g_bias.reshape(n_heads, seq_len * seq_len).T, rel_index.reshape(-1), num_segments=rel_table.shape[0])
    d_scores_bf = (d_scores * q_scale).astype(jnp.bfloat16)
    d_q_heads = jnp.einsum('nhlm,nmhe->nlhe', d_scores_bf, k_heads, preferred_element_type=jnp.float32)
    d_k_heads = jnp.einsum('nhlm,nlhe->nmhe', d_scores_bf, q_heads, preferred_element_type=jnp.float32)
    d_qkv = jnp.stack([d_q_heads, d_k_heads, d_v_heads], axis=2).reshape(-1, seq_len, 3 * model_dim)
    g_b_qkv = jnp.sum(d_qkv, axis=(0, 1))
    d_qkv_bf = d_qkv.astype(jnp.bfloat16)
    g_w_qkv = jnp.einsum('nlc,nlk->ck', normed_one, d_qkv_bf, preferred_element_type=jnp.float32)
    d_normed_one = jnp.einsum('nlk,ck->nlc', d_qkv_bf, w_qkv, preferred_element_type=jnp.float32)
    d_h_zero_ln, g_norm_attn = jax.vjp(block_norm, h_zero_f, norm_one)[1](d_normed_one)
    d_h_zero = (d_h_one + d_h_zero_ln).astype(jnp.bfloat16).reshape(n_img, win_rows, win_cols, window, window, model_dim)
    g_w_split = jnp.einsum('naprctk,nacptd->rkd', merged_in, d_h_zero, preferred_element_type=jnp.float32)
    d_merged = jnp.einsum('nacptd,rkd->naprctk', d_h_zero, w_split, preferred_element_type=jnp.float32)
    d_tok, g_norm_split = jax.vjp(merge_norm, tok_f32, norm_split)[1](d_merged)
    grad_tok = d_tok.astype(jnp.bfloat16).reshape(n_img, height, img_width, in_chans)
    g_norm_merge = g_norm_split.reshape(2, 2, 2, in_chans).transpose(0, 2, 1, 3).reshape(2, 4 * in_chans)
    g_w_reduce = g_w_split.reshape(2, 2, in_chans, model_dim).transpose(1, 0, 2, 3).reshape(4 * in_chans, model_dim)
    weight_grads = (g_norm_merge, g_w_reduce, g_norm_attn, g_w_qkv, g_b_qkv, g_rel_table, g_w_proj, g_b_proj, g_norm_mlp, g_w_fc1, g_b_fc1, g_w_fc2, g_b_fc2)
    return result, grad_tok, weight_grads


def local_step(tok_img, cot_img, rel_index, weights):
    n_img, height, img_width, in_chans = tok_img.shape
    model_dim = weights[1].shape[1]
    window = math.isqrt(rel_index.shape[0])
    merged_cols = img_width // 2
    band_count = n_img * (height // (2 * window))
    band_rows = rows_per_step(band_count, window * merged_cols)
    tok_bands = tok_img.reshape(band_count, 2 * window, img_width, in_chans)
    cot_bands = cot_img.reshape(band_count, window, merged_cols, model_dim)

    def loop_body(step_idx, carry):
        out_acc, grad_acc, wgrad_acc = carry
        start_row = step_idx * band_rows
        tok_blk = lax.dynamic_slice_in_dim(tok_bands, start_row, band_rows, axis=0)
        cot_blk = lax.dynamic_slice_in_dim(cot_bands, start_row, band_rows, axis=0)
        out_blk, grad_blk, wgrad_blk = block_step(tok_blk, cot_blk, rel_index, weights)
        out_acc = lax.dynamic_update_slice_in_dim(out_acc, out_blk, start_row, axis=0)
        grad_acc = lax.dynamic_update_slice_in_dim(grad_acc, grad_blk, start_row, axis=0)
        wgrad_acc = tuple(total_grad + step_grad for total_grad, step_grad in zip(wgrad_acc, wgrad_blk))
        return out_acc, grad_acc, wgrad_acc

    start_carry = (jnp.zeros(cot_bands.shape, jnp.bfloat16), jnp.zeros(tok_bands.shape, jnp.bfloat16), tuple(jnp.zeros(weight.shape, jnp.float32) for weight in weights))
    out_bands, grad_bands, weight_grads = lax.fori_loop(0, band_count // band_rows, loop_body, start_carry)
    return out_bands.reshape(n_img, height // 2, merged_cols, model_dim), grad_bands.reshape(tok_img.shape), weight_grads


def solution(mesh):
    def device_fn(tokens, grad_out, rel_index, *weights):
        tok_img = lax.all_to_all(tokens, 'sp', 0, 1, tiled=True)
        result, grad_img, grads_local = local_step(tok_img, grad_out, rel_index, weights)
        grad_tokens = lax.all_to_all(grad_img, 'sp', 1, 0, tiled=True)
        grads_total = lax.psum(grads_local, ('dp', 'sp'))
        return (result, grad_tokens) + tuple(grads_total)

    rep_specs = (P(),) * 13
    return jax.shard_map(device_fn, mesh=mesh, in_specs=(P('dp', 'sp'), P(('dp', 'sp')), P()) + rep_specs, out_specs=(P(('dp', 'sp')), P('dp', 'sp')) + rep_specs, check_vma=False)
```

profile of v0, /device:TPU:0, one launch (start us, length us, event | category | flops | bytes accessed | tf_op | source)
XLA Modules:
  0.0 1236.0 jit_solution(830910549934906160)
XLA Ops:
  13.8 27.0 %all-to-all-done = bf16[4,24,48,256]{3,2,1,0:T(8,128)(2,1)} async-done(((bf16[4,24,48,256]{3,2,1,0:T(8,128)(2,1)}), bf16[4,24,48,256]{3,2,1,0:T(8,128)(2,1)}, u32[]{:S(2)}, u32[]{:S(2)}) %all-to-all-start) | async-done | bytes 2359328 | tf_op jit(solution)/shard_map/all_to_all | solution.py:142
  44.3 772.6 %while.43 = (s32[]{:T(128)}, bf16[4,12,24,512]{3,2,1,0:T(8,128)(2,1)}, bf16[4,24,48,256]{3,2,1,0:T(8,128)(2,1)}, f32[2,1024]{1,0:T(2,128)}, f32[1024,512]{1,0:T(...) while((s32[]{:T(128)}, ...), condition=%wide.wide.region_28.29_spmd.clone, body=%wide.wide.region_0.28_spmd.clone.sunk | while | flops 13414966272 | bytes 569307904 | solution.py:136
  81.5 42.0 %gather_fusion = bf16[20736,16]{1,0:T(8,128)(2,1)} fusion(bf16[529,16]{1,0:T(8,128)(2,1)S(1)} %get-tuple-element.1497, s32[21504]{0:T(1024)S(1)} %pad_clamp_fusion.3), kind=kCustom, calls=%fused_computation.clone.clone.clone.1 | custom fusion | bytes 1410048 | tf_op jit(solution)/shard_map/while/body/eval_jaxpr/jit(_take)/gather | solution.py:52
  123.6 12.8 %select_convert_fusion.3 = f32[20736,16]{1,0:T(8,128)} fusion(bf16[20736,16]{1,0:T(8,128)(2,1)} %gather_fusion, pred[20736]{0:T(1024)(128)(4,1)S(1)} %compare_and_fusion.3), kind=kLoop, calls=%fused_computation.13.clone.clone.1 | loop fusion | flops 663552 | bytes 2011392 | tf_op jit(solution)/shard_map/while/body/eval_jaxpr/add | solution.py:60
  136.4 12.6 %copy.409 = f32[16,144,144]{1,2,0:T(8,128)} copy(f32[16,144,144]{0,2,1:T(8,128)} %bitcast.419) | data formatting | bytes 2654208 | tf_op jit(solution)/shard_map/while/body/eval_jaxpr/add | solution.py:60
  148.9 9.4 fusion.270
  168.0 12.3 multiply_convert_fusion.16
  187.3 7.4 fusion.277
  222.4 16.6 %fusion.284 = f32[4,144,1,16,32]{1,4,3,0,2:T(8,128)} fusion(bf16[4,144,3,16,32]{1,4,3,2,0:T(8,128)(2,1)} %bitcast.423, f32[4,16,144,144]{2,3,1,0:T(8,128)} %fusion.282, f32[4,16,144,144]{2,3,1,0:T(8,128)} %get-tuple-element.1364, f32[4,16,144]{2,1,0:T(8,128)S(1)} %get-tuple-element.1365), kind=kOutput, calls=%fused_computation.79.clone.clone.1 | convolution fusion | flops 94233744 | bytes 40108032 | tf_op jit(solution)/shard_map/while/body/eval_jaxpr/nhlm,nmhe->nlhe/dot_general | solution.py:95
  239.0 16.2 %fusion.283 = f32[4,144,1,16,32]{1,4,3,0,2:T(8,128)} fusion(bf16[4,144,3,16,32]{1,4,3,2,0:T(8,128)(2,1)} %bitcast.424, f32[4,16,144,144]{2,3,1,0:T(8,128)} %fusion.282, f32[4,16,144,144]{2,3,1,0:T(8,128)} %get-tuple-element.1364, f32[4,16,144]{2,1,0:T(8,128)S(1)} %get-tuple-element.1365), kind=kOutput, calls=%fused_computation.80.clone.clone.1 | convolution fusion | flops 94233744 | bytes 40108032 | tf_op jit(solution)/shard_map/while/body/eval_jaxpr/nhlm,nlhe->nmhe/dot_general | solution.py:96
  255.2 14.9 %fusion.292 = f32[16,144,144]{1,2,0:T(8,128)} fusion(f32[4,16,144,144]{2,3,1,0:T(8,128)} %fusion.282, f32[4,16,144,144]{2,3,1,0:T(8,128)} %get-tuple-element.1364, f32[4,16,144]{2,1,0:T(8,128)S(1)} %get-tuple-element.1365), kind=kOutput, calls=%fused_computation.177.clone.clone.1 | output fusion | flops 7640207 | bytes 11980800 | tf_op jit(solution)/shard_map/while/body/eval_jaxpr/sub | solution.py:91
  314.6 112.5 %scatter_fusion = f32[529,16]{1,0:T(8,128)S(1)} fusion(f32[529,16]{1,0:T(8,128)S(1)} %copy-done.2, s32[20736]{0:T(1024)} %get-tuple-element.1507, f32[20736,16]{1,0:T(8,128)} %copy.422), kind=kCustom, calls=%fused_computation.1.clone.clone.clone.1 | custom fusion | flops 331776 | bytes 4064256 | tf_op jit(solution)/shard_map/while/body/eval_jaxpr/scatter-add | solution.py:93
  465.1 42.0 %gather_fusion = bf16[20736,16]{1,0:T(8,128)(2,1)} fusion(bf16[529,16]{1,0:T(8,128)(2,1)S(1)} %get-tuple-element.1497, s32[21504]{0:T(1024)S(1)} %pad_clamp_fusion.3), kind=kCustom, calls=%fused_computation.clone.clone.clone.1 | custom fusion | bytes 1410048 | tf_op jit(solution)/shard_map/while/body/eval_jaxpr/jit(_take)/gather | solution.py:52
  507.1 12.8 %select_convert_fusion.3 = f32[20736,16]{1,0:T(8,128)} fusion(bf16[20736,16]{1,0:T(8,128)(2,1)} %gather_fusion, pred[20736]{0:T(1024)(128)(4,1)S(1)} %compare_and_fusion.3), kind=kLoop, calls=%fused_computation.13.clone.clone.1 | loop fusion | flops 663552 | bytes 2011392 | tf_op jit(solution)/shard_map/while/body/eval_jaxpr/add | solution.py:60
  519.9 12.4 %copy.409 = f32[16,144,144]{1,2,0:T(8,128)} copy(f32[16,144,144]{0,2,1:T(8,128)} %bitcast.419) | data formatting | bytes 2654208 | tf_op jit(solution)/shard_map/while/body/eval_jaxpr/add | solution.py:60
  532.4 9.4 fusion.270
  551.5 12.2 multiply_convert_fusion.16
  609.2 16.6 %fusion.284 = f32[4,144,1,16,32]{1,4,3,0,2:T(8,128)} fusion(bf16[4,144,3,16,32]{1,4,3,2,0:T(8,128)(2,1)} %bitcast.423, f32[4,16,144,144]{2,3,1,0:T(8,128)} %fusion.282, f32[4,16,144,144]{2,3,1,0:T(8,128)} %get-tuple-element.1364, f32[4,16,144]{2,1,0:T(8,128)S(1)} %get-tuple-element.1365), kind=kOutput, calls=%fused_computation.79.clone.clone.1 | convolution fusion | flops 94233744 | bytes 40108032 | tf_op jit(solution)/shard_map/while/body/eval_jaxpr/nhlm,nmhe->nlhe/dot_general | solution.py:95
  625.8 16.2 %fusion.283 = f32[4,144,1,16,32]{1,4,3,0,2:T(8,128)} fusion(bf16[4,144,3,16,32]{1,4,3,2,0:T(8,128)(2,1)} %bitcast.424, f32[4,16,144,144]{2,3,1,0:T(8,128)} %fusion.282, f32[4,16,144,144]{2,3,1,0:T(8,128)} %get-tuple-element.1364, f32[4,16,144]{2,1,0:T(8,128)S(1)} %get-tuple-element.1365), kind=kOutput, calls=%fused_computation.80.clone.clone.1 | convolution fusion | flops 94233744 | bytes 40108032 | tf_op jit(solution)/shard_map/while/body/eval_jaxpr/nhlm,nlhe->nmhe/dot_general | solution.py:96
  642.0 14.9 %fusion.292 = f32[16,144,144]{1,2,0:T(8,128)} fusion(f32[4,16,144,144]{2,3,1,0:T(8,128)} %fusion.282, f32[4,16,144,144]{2,3,1,0:T(8,128)} %get-tuple-element.1364, f32[4,16,144]{2,1,0:T(8,128)S(1)} %get-tuple-element.1365), kind=kOutput, calls=%fused_computation.177.clone.clone.1 | output fusion | flops 7640207 | bytes 11980800 | tf_op jit(solution)/shard_map/while/body/eval_jaxpr/sub | solution.py:91
  702.1 112.5 %scatter_fusion = f32[529,16]{1,0:T(8,128)S(1)} fusion(f32[529,16]{1,0:T(8,128)S(1)} %copy-done.2, s32[20736]{0:T(1024)} %get-tuple-element.1507, f32[20736,16]{1,0:T(8,128)} %copy.422), kind=kCustom, calls=%fused_computation.1.clone.clone.clone.1 | custom fusion | flops 331776 | bytes 4064256 | tf_op jit(solution)/shard_map/while/body/eval_jaxpr/scatter-add | solution.py:93
  820.4 31.9 %all_to_all.21 = bf16[1,96,48,256]{3,2,0,1:T(8,128)(2,1)} all-to-all(bf16[1,96,48,256]{3,2,0,1:T(8,128)(2,1)S(1)} %bitcast.440), channel_id=1, replica_groups=mesh['dp'=8,'sp'=4] {'sp'}, dimensions={1} | all-to-all | bytes 4718592 | tf_op jit(solution)/shard_map/all_to_all | solution.py:144
  852.4 98.1 %all-reduce.11.cloned.1.call-done = (f32[2,1024]{1,0:T(2,128)}, f32[2,512]{1,0:T(2,128)}, f32[1536]{0:T(1024)}, f32[529,16]{0,1:T(8,128)}, f32[512]{0:T(512)}, /...) async-done(((f32[2,1024]{1,0:T(2,128)}, f32[2,512]{1,0:T(2,128)}, f32[1536]{0:T(1024)}, f32[529,16]{0,1:T(8,128)}, f32[512]{0:T(512)}, /*index=5*/f32[2,512]{1,0:T(2,128)}, ...) | async-done | bytes 68688 | tf_op jit(solution)/shard_map/psum | solution.py:145
  950.5 261.0 %all-reduce.13.cloned.1.call-done = (f32[1024,512]{1,0:T(8,128)}, f32[512,1536]{1,0:T(8,128)}, f32[512,512]{1,0:T(8,128)}, f32[512,2048]{1,0:T(8,128)}, f32[2048,512]{1,0:T(8,128)}) async-done(((f32[1024,512]{1,0:T(8,128)}, f32[512,1536]{1,0:T(8,128)}, f32[512,512]{1,0:T(8,128)}, f32[512,2048]{1,0:T(8,128)}, f32[2048,512]{1,0:T(8,128)}), (f32[1024,512]{1,0:T(8,128)}, f32[512,1536]{1,0:T(8,128)}, ...) | async-done | bytes 14680080 | tf_op jit(solution)/shard_map/psum | solution.py:145
  (515 shorter events, 293.7 us)
Async XLA Ops:
  7.2 33.6 %all-to-all-start = ((bf16[4,24,48,256]{3,2,1,0:T(8,128)(2,1)}), bf16[4,24,48,256]{3,2,1,0:T(8,128)(2,1)}, u32[]{:S(2)}, u32[]{:S(2)}) async-start(bf16[4,24,48,256]{3,2,1,0:T(8,128)(2,1)} %param.18), calls=%async_computation | async-start | bytes 4718592 | tf_op jit(solution)/shard_map/all_to_all | solution.py:142
  11.9 32.3 %copy-start.48 = (bf16[2,512]{1,0:T(2,128)(2,1)S(1)}, bf16[2,512]{1,0:T(2,128)(2,1)}, u32[]{:S(2)}) copy-start(bf16[2,512]{1,0:T(2,128)(2,1)} %param.23) | copy-start | bytes 6148
  11.9 32.3 %copy-start.53 = (bf16[2,1024]{1,0:T(2,128)(2,1)S(1)}, bf16[2,1024]{1,0:T(2,128)(2,1)}, u32[]{:S(2)}) copy-start(bf16[2,1024]{1,0:T(2,128)(2,1)} %param.21) | copy-start | bytes 12292
  11.9 32.3 %copy-start.55 = (bf16[1536]{0:T(1024)(128)(2,1)S(1)}, bf16[1536]{0:T(1024)(128)(2,1)}, u32[]{:S(2)}) copy-start(bf16[1536]{0:T(1024)(128)(2,1)} %param.25) | copy-start | bytes 9220
  11.9 32.3 %copy-start.57 = (bf16[2048]{0:T(1024)(128)(2,1)S(1)}, bf16[2048]{0:T(1024)(128)(2,1)}, u32[]{:S(2)}) copy-start(bf16[2048]{0:T(1024)(128)(2,1)} %param.31) | copy-start | bytes 12292
  12.0 938.5 %all-reduce.11.cloned.1.call-start = ((), (), s32[]{:S(2)}) async-start(), calls=%async_computation.2 | async-start | bytes 155648 | tf_op jit(solution)/shard_map/psum | solution.py:145
  44.5 37.0 %copy-start = (bf16[529,16]{1,0:T(8,128)(2,1)}, bf16[529,16]{1,0:T(8,128)(2,1)S(1)}, u32[]{:S(2)}) copy-start(bf16[529,16]{1,0:T(8,128)(2,1)S(1)} %get-tuple-element.1497) | copy-start | bytes 50788 | tf_op jit(solution)/shard_map/while
  314.5 113.3 %copy-start.1 = (bf16[529,16]{1,0:T(8,128)(2,1)S(1)}, bf16[529,16]{1,0:T(8,128)(2,1)}, u32[]{:S(2)}) copy-start(bf16[529,16]{1,0:T(8,128)(2,1)} %copy-done) | copy-start | bytes 50788 | tf_op jit(solution)/shard_map/while
  314.5 113.3 %copy-start.49 = (bf16[2,512]{1,0:T(2,128)(2,1)S(1)}, bf16[2,512]{1,0:T(2,128)(2,1)}, u32[]{:S(2)}) copy-start(bf16[2,512]{1,0:T(2,128)(2,1)} %get-tuple-element.1624) | copy-start | bytes 6148 | tf_op jit(solution)/shard_map/while
  314.5 113.3 %copy-start.54 = (bf16[2,1024]{1,0:T(2,128)(2,1)S(1)}, bf16[2,1024]{1,0:T(2,128)(2,1)}, u32[]{:S(2)}) copy-start(bf16[2,1024]{1,0:T(2,128)(2,1)} %get-tuple-element.1668) | copy-start | bytes 12292 | tf_op jit(solution)/shard_map/while
  314.5 113.3 %copy-start.56 = (bf16[1536]{0:T(1024)(128)(2,1)S(1)}, bf16[1536]{0:T(1024)(128)(2,1)}, u32[]{:S(2)}) copy-start(bf16[1536]{0:T(1024)(128)(2,1)} %get-tuple-element.1710) | copy-start | bytes 9220 | tf_op jit(solution)/shard_map/while
  314.5 113.3 %copy-start.58 = (bf16[2048]{0:T(1024)(128)(2,1)S(1)}, bf16[2048]{0:T(1024)(128)(2,1)}, u32[]{:S(2)}) copy-start(bf16[2048]{0:T(1024)(128)(2,1)} %get-tuple-element.1753) | copy-start | bytes 12292 | tf_op jit(solution)/shard_map/while
  314.5 113.3 %copy-start.63 = (bf16[512]{0:T(512)(128)(2,1)S(1)}, bf16[512]{0:T(512)(128)(2,1)}, u32[]{:S(2)}) copy-start(bf16[512]{0:T(512)(128)(2,1)} %get-tuple-element.1801) | copy-start | bytes 3076 | tf_op jit(solution)/shard_map/while
  314.5 113.3 %copy-start.65 = (bf16[512]{0:T(512)(128)(2,1)S(1)}, bf16[512]{0:T(512)(128)(2,1)}, u32[]{:S(2)}) copy-start(bf16[512]{0:T(512)(128)(2,1)} %get-tuple-element.1846) | copy-start | bytes 3076 | tf_op jit(solution)/shard_map/while
  428.0 37.0 %copy-start = (bf16[529,16]{1,0:T(8,128)(2,1)}, bf16[529,16]{1,0:T(8,128)(2,1)S(1)}, u32[]{:S(2)}) copy-start(bf16[529,16]{1,0:T(8,128)(2,1)S(1)} %get-tuple-element.1497) | copy-start | bytes 50788 | tf_op jit(solution)/shard_map/while
  702.0 113.3 %copy-start.1 = (bf16[529,16]{1,0:T(8,128)(2,1)S(1)}, bf16[529,16]{1,0:T(8,128)(2,1)}, u32[]{:S(2)}) copy-start(bf16[529,16]{1,0:T(8,128)(2,1)} %copy-done) | copy-start | bytes 50788 | tf_op jit(solution)/shard_map/while
  702.0 113.3 %copy-start.49 = (bf16[2,512]{1,0:T(2,128)(2,1)S(1)}, bf16[2,512]{1,0:T(2,128)(2,1)}, u32[]{:S(2)}) copy-start(bf16[2,512]{1,0:T(2,128)(2,1)} %get-tuple-element.1624) | copy-start | bytes 6148 | tf_op jit(solution)/shard_map/while
  702.0 113.3 %copy-start.54 = (bf16[2,1024]{1,0:T(2,128)(2,1)S(1)}, bf16[2,1024]{1,0:T(2,128)(2,1)}, u32[]{:S(2)}) copy-start(bf16[2,1024]{1,0:T(2,128)(2,1)} %get-tuple-element.1668) | copy-start | bytes 12292 | tf_op jit(solution)/shard_map/while
  702.0 113.3 %copy-start.56 = (bf16[1536]{0:T(1024)(128)(2,1)S(1)}, bf16[1536]{0:T(1024)(128)(2,1)}, u32[]{:S(2)}) copy-start(bf16[1536]{0:T(1024)(128)(2,1)} %get-tuple-element.1710) | copy-start | bytes 9220 | tf_op jit(solution)/shard_map/while
  702.0 113.3 %copy-start.58 = (bf16[2048]{0:T(1024)(128)(2,1)S(1)}, bf16[2048]{0:T(1024)(128)(2,1)}, u32[]{:S(2)}) copy-start(bf16[2048]{0:T(1024)(128)(2,1)} %get-tuple-element.1753) | copy-start | bytes 12292 | tf_op jit(solution)/shard_map/while
  702.1 113.3 %copy-start.63 = (bf16[512]{0:T(512)(128)(2,1)S(1)}, bf16[512]{0:T(512)(128)(2,1)}, u32[]{:S(2)}) copy-start(bf16[512]{0:T(512)(128)(2,1)} %get-tuple-element.1801) | copy-start | bytes 3076 | tf_op jit(solution)/shard_map/while
  702.1 113.3 %copy-start.65 = (bf16[512]{0:T(512)(128)(2,1)S(1)}, bf16[512]{0:T(512)(128)(2,1)}, u32[]{:S(2)}) copy-start(bf16[512]{0:T(512)(128)(2,1)} %get-tuple-element.1846) | copy-start | bytes 3076 | tf_op jit(solution)/shard_map/while
  818.7 392.8 %all-reduce.13.cloned.1.call-start = ((), (), s32[]{:S(2)}) async-start(), calls=%async_computation.3 | async-start | bytes 29360128 | tf_op jit(solution)/shard_map/psum | solution.py:145
  950.5 264.4 %copy-start.69 = (f32[2,1024]{1,0:T(2,128)S(1)}, f32[2,1024]{1,0:T(2,128)}, u32[]{:S(2)}) copy-start(f32[2,1024]{1,0:T(2,128)} %get-tuple-element.1530) | copy-start | bytes 24580
  (117 other events, 511.8 us)
Sparse Core Ops, SparseCore 0:
  818.8 131.6 all-reduce.10
  958.1 253.3 all-reduce.12
where the time goes:
time: 1240 us
  waiting for transfers between devices  387 us (31%)
  other arithmetic  350 us (28%)
  local copies, waits for them, and re-layouts  247 us (20%)
  matrix products  198 us (16%)
  blocking collectives  31.9 us (3%)
  between operations  14.5 us (1%)
    psum x2, waiting for transfers between devices, device_fn(): grads_total = lax.psum(grads_local, ('dp', 'sp'))  359 us
    scatter-add x2, other arithmetic, block_step(): jax.ops.segment_sum(g_bias.reshape(n_heads, seq_len * seq_len).T, rel_ind...  225 us
    gather x2, local copies, waits for them, and re-layouts, block_step(): jnp.take(rel_table, rel_index.reshape(-1), axis=0).astype(jnp.float32)  84.1 us
    dot_general x2, matrix products, block_step(): jnp.einsum('nhlm,nmhe->nlhe', d_scores_bf, k_heads, preferred_element_typ...  33.1 us
    dot_general x2, matrix products, block_step(): jnp.einsum('nhlm,nlhe->nmhe', d_scores_bf, q_heads, preferred_element_typ...  32.4 us
    all_to_all x1, blocking collectives, device_fn(): grad_tokens = lax.all_to_all(grad_img, 'sp', 1, 0, tiled=True)  31.9 us
    sub x2, other arithmetic, block_step(): d_prob - jnp.sum(d_prob * attn_prob, axis=-1, keepdims=True)  29.8 us
    all_to_all x1, waiting for transfers between devices, device_fn(): tok_img = lax.all_to_all(tokens, 'sp', 0, 1, tiled=True)  27 us
  transfers between devices with their start and end apart: 3, of which 3 were waited for; matrix products, arithmetic and copies ran while one was open for 0% of the time, Pallas kernels for 0%

commit v1 on v0

v1 whole, which is shorter than its diff:
```python
import functools
import math
import numpy as np
import jax
import jax.numpy as jnp
from jax import lax
from jax.experimental import pallas as pl
from jax.experimental.pallas import tpu as pltpu
from jax.sharding import PartitionSpec as P

NORM_EPS = 1e-5
BF, F32 = jnp.bfloat16, jnp.float32
VMEM_LIMIT = 60 * 1024 * 1024
HEAD_GROUP = 8
GROUP_ROWS = 4


def dot_nn(a, b):
    return lax.dot_general(a, b, (((1,), (0,)), ((), ())), preferred_element_type=F32)


def dot_nt(a, b):
    return lax.dot_general(a, b, (((1,), (1,)), ((), ())), preferred_element_type=F32)


def dot_tn(a, b):
    return lax.dot_general(a, b, (((0,), (0,)), ((), ())), preferred_element_type=F32)


def norm_hat(x):
    mu = jnp.mean(x, axis=-1, keepdims=True)
    xc = x - mu
    rstd = lax.rsqrt(jnp.mean(xc * xc, axis=-1, keepdims=True) + NORM_EPS)
    return xc * rstd, rstd


def norm_fwd(x, norm_ref):
    hat, rstd = norm_hat(x)
    return hat * norm_ref[0:1, :].astype(F32) + norm_ref[1:2, :].astype(F32), hat, rstd


def norm_bwd(dy, hat, rstd, norm_ref):
    dhat = dy * norm_ref[0:1, :].astype(F32)
    m1 = jnp.mean(dhat, axis=-1, keepdims=True)
    m2 = jnp.mean(dhat * hat, axis=-1, keepdims=True)
    dx = rstd * (dhat - m1 - hat * m2)
    return dx, jnp.sum(dy * hat, axis=0, keepdims=True), jnp.sum(dy, axis=0, keepdims=True)


def head_masks(width, head_dim, dtype):
    lane = lax.broadcasted_iota(jnp.int32, (1, width), 1) // head_dim
    return [jnp.where(lane == h, 1.0, 0.0).astype(dtype) for h in range(width // head_dim)]


def stack_heads(x, masks):
    return jnp.concatenate([x * m for m in masks], axis=0)


def unstack_heads(x, masks, seq):
    total = x[0:seq] * masks[0]
    for h in range(1, len(masks)):
        total = total + x[h * seq:(h + 1) * seq] * masks[h]
    return total


def pos_kernel(table_ref, idx_ref, pos_ref):
    seq = idx_ref.shape[0]
    n_pieces = table_ref.shape[1] // 128
    for g in range(pos_ref.shape[0]):
        wide = jnp.concatenate([idx_ref[...]] * HEAD_GROUP, axis=1)
        for c in range(wide.shape[1] // 128):
            idx = wide[:, c * 128:(c + 1) * 128]
            low, high = idx & 127, idx >> 7
            lane = lax.broadcasted_iota(jnp.int32, idx.shape, 1) + c * 128
            out = jnp.zeros(idx.shape, F32)
            for h in range((c * 128) // seq, (c * 128 + 127) // seq + 1):
                val = jnp.zeros(idx.shape, F32)
                for t in range(n_pieces):
                    row = table_ref[g * HEAD_GROUP + h:g * HEAD_GROUP + h + 1, t * 128:(t + 1) * 128]
                    got = jnp.take_along_axis(jnp.broadcast_to(row, idx.shape), low, axis=1)
                    val = jnp.where(high == t, got, val)
                out = jnp.where((lane >= h * seq) & (lane < (h + 1) * seq), val, out)
            pos_ref[g, :, c * 128:(c + 1) * 128] = out


def fwd_kernel(tok_ref, perm_ref, pos_ref, nm_ref, wr_ref, na_ref, wq_ref, bq_ref, wp_ref, bp_ref,
               raw_ref, h0_ref, qkv_ref, att_ref, lse_ref, h1_ref, *, head_dim, seq):
    dim = h0_ref.shape[2]
    x = tok_ref[0].reshape(-1, tok_ref.shape[3])
    step = perm_ref.shape[0]
    quad = step // 4
    piece = quad // 2
    for g in range(x.shape[0] // step):
        y = dot_nn(perm_ref[...], x[g * step:(g + 1) * step])
        for w in range(2):
            cat = jnp.concatenate([y[p * quad + w * piece:p * quad + (w + 1) * piece] for p in range(4)], axis=1)
            raw_ref[0, w * seq + g * piece:w * seq + (g + 1) * piece, :] = cat.astype(BF)
    merged = norm_fwd(raw_ref[0].astype(F32), nm_ref)[0].astype(BF)
    h0 = dot_nn(merged, wr_ref[...]).astype(BF)
    h0_ref[0] = h0
    a = norm_fwd(h0.astype(F32), na_ref)[0].astype(BF)
    qkv_ref[0] = (dot_nn(a, wq_ref[...]) + bq_ref[...].astype(F32)).astype(BF)
    width = HEAD_GROUP * head_dim
    masks, masks_f = head_masks(width, head_dim, BF), head_masks(width, head_dim, F32)
    scale = head_dim ** -0.5
    for w in range(2):
        rows = slice(w * seq, (w + 1) * seq)
        for g in range(dim // width):
            cols = [slice(t * dim + g * width, t * dim + (g + 1) * width) for t in range(3)]
            q, k, v = (qkv_ref[0, rows, c] for c in cols)
            s = dot_nt(k, stack_heads(q, masks)) * scale + pos_ref[g]
            top = jnp.max(s, axis=0, keepdims=True)
            e = jnp.exp(s - top)
            den = jnp.sum(e, axis=0, keepdims=True)
            prob = (e * (1.0 / den)).astype(BF)
            lse_ref[0, w, g] = top + jnp.log(den)
            att_ref[0, rows, g * width:(g + 1) * width] = unstack_heads(dot_tn(prob, v), masks_f, seq).astype(BF)
    h1 = h0_ref[0].astype(F32) + dot_nn(att_ref[0], wp_ref[...]) + bp_ref[...].astype(F32)
    h1_ref[0] = h1.astype(BF)


def mlp_kernel(h1_ref, cot_ref, perm_ref, nb_ref, w1_ref, b1_ref, w2_ref, b2_ref,
               out_ref, dh1_ref, gw1_ref, gw2_ref, gb1_ref, gb2_ref, gnb_ref,
               hid_s, dpre_s, b_s, cot_s):
    i = pl.program_id(0)
    n = h1_ref.shape[1]

    @pl.when(i == 0)
    def _():
        gb1_ref[...] = jnp.zeros(gb1_ref.shape, F32)
        gb2_ref[...] = jnp.zeros(gb2_ref.shape, F32)
        gnb_ref[...] = jnp.zeros(gnb_ref.shape, F32)

    rows = pl.ds(pl.multiple_of(i * n, n), n)
    h1 = h1_ref[0].astype(F32)
    normed, hat, rstd = norm_fwd(h1, nb_ref)
    nb = normed.astype(BF)
    b_s[rows, :] = nb
    cot = dot_nn(perm_ref[...], cot_ref[0])
    cot_bf = cot.astype(BF)
    cot_s[rows, :] = cot_bf
    gb2_ref[...] += jnp.sum(cot, axis=0, keepdims=True)
    out = h1 + b2_ref[...].astype(F32)
    d_norm = jnp.zeros(h1.shape, F32)
    chunk = 512
    for c in range(w1_ref.shape[1] // chunk):
        cols = slice(c * chunk, (c + 1) * chunk)
        pre = dot_nn(nb, w1_ref[:, cols]) + b1_ref[:, cols].astype(F32)
        phi = 0.5 + 0.5 * lax.erf(pre * math.sqrt(0.5))
        hid = (pre * phi).astype(BF)
        hid_s[rows, cols] = hid
        out = out + dot_nn(hid, w2_ref[cols, :])
        d_act = phi + pre * (jnp.exp(pre * pre * -0.5) * (1.0 / math.sqrt(2.0 * math.pi)))
        d_pre = dot_nt(cot_bf, w2_ref[cols, :]) * d_act
        gb1_ref[:, cols] += jnp.sum(d_pre, axis=0, keepdims=True)
        d_pre_bf = d_pre.astype(BF)
        dpre_s[rows, cols] = d_pre_bf
        d_norm = d_norm + dot_nt(d_pre_bf, w1_ref[:, cols])
    out_ref[0] = dot_tn(perm_ref[...], out.astype(BF)).astype(BF)
    dx, g_gain, g_shift = norm_bwd(d_norm, hat, rstd, nb_ref)
    gnb_ref[0:1, :] += g_gain
    gnb_ref[1:2, :] += g_shift
    dh1_ref[0] = cot + dx

    @pl.when(i == pl.num_programs(0) - 1)
    def _():
        def body(c, carry):
            cols = pl.ds(pl.multiple_of(c * chunk, chunk), chunk)
            gw1_ref[:, cols] = dot_tn(b_s[...], dpre_s[:, cols])
            gw2_ref[cols, :] = dot_tn(hid_s[:, cols], cot_s[...])
            return carry
        lax.fori_loop(0, w1_ref.shape[1] // chunk, body, 0)


def bwd_kernel(dh1_ref, raw_ref, h0_ref, qkv_ref, att_ref, lse_ref, perm_ref, pos_ref, nm_ref, wr_ref, na_ref, wq_ref, wp_ref,
               gtok_ref, gwp_ref, gwq_ref, gwr_ref, gbp_ref, gbq_ref, gna_ref, gnm_ref, gpos_ref,
               att_s, dh1_s, a_s, dqkv_s, m_s, dh0_s, datt_s, dqkv_f, *, head_dim, seq):
    i = pl.program_id(0)
    n = dh1_ref.shape[1]
    dim = h0_ref.shape[2]

    @pl.when(i == 0)
    def _():
        for ref in (gbp_ref, gbq_ref, gna_ref, gnm_ref, gpos_ref):
            ref[...] = jnp.zeros(ref.shape, F32)

    here = pl.ds(pl.multiple_of(i * n, n), n)
    dh1 = dh1_ref[0]
    gbp_ref[...] += jnp.sum(dh1, axis=0, keepdims=True)
    dh1_bf = dh1.astype(BF)
    dh1_s[here, :] = dh1_bf
    att_s[here, :] = att_ref[0]
    datt_s[...] = dot_nt(dh1_bf, wp_ref[...]).astype(BF)
    width = HEAD_GROUP * head_dim
    masks, masks_f = head_masks(width, head_dim, BF), head_masks(width, head_dim, F32)
    scale = head_dim ** -0.5
    for w in range(2):
        rows = slice(w * seq, (w + 1) * seq)
        for g in range(dim // width):
            cols = [slice(t * dim + g * width, t * dim + (g + 1) * width) for t in range(3)]
            q, k, v = (qkv_ref[0, rows, c] for c in cols)
            qm = stack_heads(q, masks)
            dam = stack_heads(datt_s[rows, g * width:(g + 1) * width], masks)
            prob = jnp.exp(dot_nt(k, qm) * scale + pos_ref[g] - lse_ref[0, w, g])
            d_prob = dot_nt(v, dam)
            dqkv_f[rows, cols[2]] = dot_nn(prob.astype(BF), dam)
            delta = jnp.sum(d_prob * prob, axis=0, keepdims=True)
            ds = prob * (d_prob - delta)
            gpos_ref[g] += ds
            ds_bf = (ds * scale).astype(BF)
            dqkv_f[rows, cols[1]] = dot_nn(ds_bf, qm)
            dqkv_f[rows, cols[0]] = unstack_heads(dot_tn(ds_bf, k), masks_f, seq)
    gbq_ref[...] += jnp.sum(dqkv_f[...], axis=0, keepdims=True)
    dqkv_bf = dqkv_f[...].astype(BF)
    dqkv_s[here, :] = dqkv_bf
    d_a = dot_nt(dqkv_bf, wq_ref[...])
    normed, hat, rstd = norm_fwd(h0_ref[0].astype(F32), na_ref)
    a_s[here, :] = normed.astype(BF)
    dx, g_gain, g_shift = norm_bwd(d_a, hat, rstd, na_ref)
    gna_ref[0:1, :] += g_gain
    gna_ref[1:2, :] += g_shift
    dh0_bf = (dh1 + dx).astype(BF)
    dh0_s[here, :] = dh0_bf
    d_m = dot_nt(dh0_bf, wr_ref[...])
    normed, hat, rstd = norm_fwd(raw_ref[0].astype(F32), nm_ref)
    m_s[here, :] = normed.astype(BF)
    dx, g_gain, g_shift = norm_bwd(d_m, hat, rstd, nm_ref)
    gnm_ref[0:1, :] += g_gain
    gnm_ref[1:2, :] += g_shift
    d_raw = dx.astype(BF)
    step = perm_ref.shape[0]
    quad = step // 4
    piece = quad // 2
    chan = d_raw.shape[1] // 4
    tok_rows = step // gtok_ref.shape[2]
    for g in range(seq // piece):
        y = jnp.concatenate([d_raw[w * seq + g * piece:w * seq + (g + 1) * piece, p * chan:(p + 1) * chan]
                             for p in range(4) for w in range(2)], axis=0)
        gtok_ref[0, g * tok_rows:(g + 1) * tok_rows] = dot_tn(perm_ref[...], y).astype(BF).reshape(tok_rows, gtok_ref.shape[2], chan)

    @pl.when(i == pl.num_programs(0) - 1)
    def _():
        gwp_ref[...] = dot_tn(att_s[...], dh1_s[...])

        def body_q(c, carry):
            cols = pl.ds(pl.multiple_of(c * 512, 512), 512)
            gwq_ref[:, cols] = dot_tn(a_s[...], dqkv_s[:, cols])
            return carry
        lax.fori_loop(0, gwq_ref.shape[1] // 512, body_q, 0)

        def body_r(c, carry):
            cols = pl.ds(pl.multiple_of(c * 512, 512), 512)
            gwr_ref[cols, :] = dot_tn(m_s[:, cols], dh0_s[...])
            return carry
        lax.fori_loop(0, gwr_ref.shape[0] // 512, body_r, 0)


def table_kernel(gpos_ref, idx_ref, out_ref, parts_s, *, n_heads):
    m0 = pl.program_id(0)
    count = idx_ref.shape[0]

    @pl.when(m0 == 0)
    def _():
        out_ref[...] = jnp.zeros(out_ref.shape, F32)
    acc = jnp.zeros(out_ref.shape, F32)
    row = lax.broadcasted_iota(jnp.int32, (out_ref.shape[1], idx_ref.shape[1]), 0)
    for j in range(count):
        hot = jnp.where(row == idx_ref[j:j + 1, :], 1.0, 0.0).astype(BF)
        val = gpos_ref[j]
        hi = val.astype(BF)
        rest = val - hi.astype(F32)
        mid = rest.astype(BF)
        low = (rest - mid.astype(F32)).astype(BF)
        acc = acc + dot_nt(jnp.concatenate([hi, mid, low], axis=0), hot)
    out_ref[...] += acc


def whole(shape):
    zeros = (0,) * len(shape)
    return pl.BlockSpec(shape, lambda i: zeros, pipeline_mode=pl.Buffered(1))


def out_whole(shape):
    zeros = (0,) * len(shape)
    return pl.BlockSpec(shape, lambda i: zeros)


def band(shape):
    zeros = (0,) * (len(shape) - 1)
    return pl.BlockSpec((1,) + shape[1:], lambda i: (i,) + zeros)


def sds(shape, dtype):
    return jax.ShapeDtypeStruct(shape, dtype)


def call(kernel, grid, ins, in_specs, outs, out_specs, scratch, flops, name):
    moved = sum(math.prod(a.shape) * a.dtype.itemsize for a in list(ins) + list(outs))
    return pl.pallas_call(
        kernel, grid=grid, in_specs=in_specs, out_specs=out_specs, out_shape=outs, scratch_shapes=scratch, name=name,
        cost_estimate=pl.CostEstimate(flops=flops, bytes_accessed=moved, transcendentals=0),
        compiler_params=pltpu.CompilerParams(vmem_limit_bytes=VMEM_LIMIT, dimension_semantics=("arbitrary",) * len(grid)))(*ins)


def merge_perm(window, cols):
    rows_in = 2 * GROUP_ROWS * cols
    perm = np.zeros((rows_in, rows_in), np.float32)
    out = 0
    for quad in range(4):
        c, r = quad // 2, quad % 2
        for w in range(2):
            for i in range(GROUP_ROWS):
                for j in range(window):
                    perm[out, (2 * i + r) * cols + 2 * (w * window + j) + c] = 1.0
                    out += 1
    return jnp.asarray(perm, BF)


def window_perm(window):
    n = 2 * window * window
    perm = np.zeros((n, n), np.float32)
    for w in range(2):
        for i in range(window):
            for j in range(window):
                perm[(w * window + i) * window + j, (i * 2 + w) * window + j] = 1.0
    return jnp.asarray(perm, BF)


def local_step(tokens, cot, rel_index, weights):
    (norm_merge, w_reduce, norm_attn, w_qkv, b_qkv, rel_table, w_proj, b_proj, norm_mlp, w_fc1, b_fc1, w_fc2, b_fc2) = weights
    nb, tok_rows, tok_cols, chan = tokens.shape
    dim = w_reduce.shape[1]
    ff = w_fc1.shape[1]
    n_heads = rel_table.shape[1]
    head_dim = dim // n_heads
    seq = rel_index.shape[0]
    window = math.isqrt(seq)
    n = 2 * seq
    groups = n_heads // HEAD_GROUP
    lanes = HEAD_GROUP * seq
    table_pad = -(-rel_table.shape[0] // 128) * 128
    perm4, perm_w = merge_perm(window, tok_cols), window_perm(window)
    table_t = jnp.pad(rel_table.astype(F32).T, ((0, 0), (0, table_pad - rel_table.shape[0])))
    idx_t = rel_index.T
    row = lambda x: x.reshape(1, -1)

    pos = call(pos_kernel, (1,), (table_t, idx_t), [whole(table_t.shape), whole(idx_t.shape)],
               [sds((groups, seq, lanes), F32)], [out_whole((groups, seq, lanes))], [], 10**7, "pos")[0]

    ins = (tokens, perm4, pos, norm_merge, w_reduce, norm_attn, w_qkv, row(b_qkv), w_proj, row(b_proj))
    outs = [sds((nb, n, 4 * chan), BF), sds((nb, n, dim), BF), sds((nb, n, 3 * dim), BF), sds((nb, n, dim), BF),
            sds((nb, 2, groups, 1, lanes), F32), sds((nb, n, dim), BF)]
    raw, h0, qkv, att, lse, h1 = call(
        functools.partial(fwd_kernel, head_dim=head_dim, seq=seq), (nb,), ins,
        [band(tokens.shape)] + [whole(a.shape) for a in ins[1:]], outs, [band(o.shape) for o in outs], [], 8 * 10**9, "fwd")

    ins = (h1, cot.reshape(nb, n, dim), perm_w, norm_mlp, w_fc1, row(b_fc1), w_fc2, row(b_fc2))
    outs = [sds((nb, n, dim), BF), sds((nb, n, dim), F32), sds((dim, ff), F32), sds((ff, dim), F32), sds((1, ff), F32), sds((1, dim), F32), sds((2, dim), F32)]
    result, dh1, g_w1, g_w2, g_b1, g_b2, g_nb = call(
        mlp_kernel, (nb,), ins, [band(ins[0].shape), band(ins[1].shape)] + [whole(a.shape) for a in ins[2:]],
        outs, [band(outs[0].shape), band(outs[1].shape)] + [out_whole(o.shape) for o in outs[2:]],
        [pltpu.VMEM((nb * n, ff), BF), pltpu.VMEM((nb * n, ff), BF), pltpu.VMEM((nb * n, dim), BF), pltpu.VMEM((nb * n, dim), BF)],
        16 * 10**9, "mlp")

    ins = (dh1, raw, h0, qkv, att, lse, perm4, pos, norm_merge, w_reduce, norm_attn, w_qkv, w_proj)
    outs = [sds(tokens.shape, BF), sds((dim, dim), F32), sds((dim, 3 * dim), F32), sds((4 * chan, dim), F32), sds((1, dim), F32),
            sds((1, 3 * dim), F32), sds((2, dim), F32), sds((2, 4 * chan), F32), sds((groups, seq, lanes), F32)]
    g_tok, g_wp, g_wq, g_wr, g_bp, g_bq, g_na, g_nm, g_pos = call(
        functools.partial(bwd_kernel, head_dim=head_dim, seq=seq), (nb,), ins,
        [band(a.shape) for a in ins[:6]] + [whole(a.shape) for a in ins[6:]],
        outs, [band(outs[0].shape)] + [out_whole(o.shape) for o in outs[1:]],
        [pltpu.VMEM((nb * n, dim), BF), pltpu.VMEM((nb * n, dim), BF), pltpu.VMEM((nb * n, dim), BF), pltpu.VMEM((nb * n, 3 * dim), BF),
         pltpu.VMEM((nb * n, 4 * chan), BF), pltpu.VMEM((nb * n, dim), BF), pltpu.VMEM((n, dim), BF), pltpu.VMEM((n, 3 * dim), F32)],
        16 * 10**9, "bwd")

    g_pos = g_pos.reshape(groups, seq, HEAD_GROUP, seq).transpose(1, 0, 2, 3).reshape(seq, n_heads, seq)
    block = 8
    parts = call(functools.partial(table_kernel, n_heads=n_heads), (seq // block,), (g_pos, idx_t),
                 [pl.BlockSpec((block, n_heads, seq), lambda i: (i, 0, 0)), pl.BlockSpec((block, seq), lambda i: (i, 0))],
                 [sds((3 * n_heads, table_pad), F32)], [out_whole((3 * n_heads, table_pad))], [pltpu.VMEM((8, 128), F32)], 10**9, "table")[0]
    g_table = parts.reshape(3, n_heads, table_pad).sum(0).T[:rel_table.shape[0]]
    return result, g_tok, (g_nm, g_wr, g_na, g_wq, g_bq[0], g_table, g_wp, g_bp[0], g_nb, g_w1, g_b1[0], g_w2, g_b2[0])


def solution(mesh):
    def device_fn(tokens, grad_out, rel_index, *weights):
        nb = mesh.shape['sp']
        cot = lax.all_to_all(grad_out, 'sp', 1, 0, tiled=True)
        result, g_tok, grads = local_step(tokens, cot, rel_index, weights)
        result = lax.all_to_all(result.reshape(cot.shape), 'sp', 0, 1, tiled=True)
        total = lax.psum(grads, ('dp', 'sp'))
        return (result, g_tok) + tuple(total)

    rep_specs = (P(),) * 13
    return jax.shard_map(device_fn, mesh=mesh, in_specs=(P('dp', 'sp'), P(('dp', 'sp')), P()) + rep_specs, out_specs=(P(('dp', 'sp')), P('dp', 'sp')) + rep_specs, check_vma=False)
```

time: 1240 us -> 553 us (0.45)
  other arithmetic: 350 us -> 2.77 us
  local copies, waits for them, and re-layouts: 247 us -> 24.5 us
  matrix products: 198 us -> 0 us
  Pallas kernels: 0 us -> 112 us
  waiting for transfers between devices: 387 us -> 374 us
    scatter-add x2 -> x0, other arithmetic: 225 us -> none  [block_step(): jax.ops.segment_sum(g_bias.reshape(n_heads, seq_len * seq_len).T, rel_ind...]
    dot_general x40 -> x0, matrix products: 179 us -> none  [the longest x2 33.1 us: block_step(): jnp.einsum('nhlm,nmhe->nlhe', d_scores_bf, k_heads, preferred_element_typ...]
    pallas_call x0 -> x5, Pallas kernels: none -> 112 us  [call(): pl.pallas_call(kernel, grid=grid, in_specs=in_specs, out_specs=out_specs,...]
    gather x2 -> x0, local copies, waits for them, and re-layouts: 84.1 us -> none  [block_step(): jnp.take(rel_table, rel_index.reshape(-1), axis=0).astype(jnp.float32)]
    convert_element_type x18 -> x0, other arithmetic: 37.6 us -> none  [the longest x2 24.5 us: block_step(): hidden = jax.nn.gelu(pre_act, approximate=False).astype(jnp.bfloat16)]
    convert_element_type x22 -> x0, local copies, waits for them, and re-layouts: 36.7 us -> none  [the longest x4 10.7 us: block_step(): tok_img.reshape(n_img, win_rows, window, 2, win_cols, window, 2 * in_chans)]
    add x20 -> x0, other arithmetic: 31.3 us -> none  [the longest x2 25.7 us: block_step(): jnp.einsum('nlhe,nmhe->nhlm', q_heads, k_heads, preferred_element_type=jn...]
    sub x2 -> x0, other arithmetic: 29.8 us -> none  [block_step(): d_prob - jnp.sum(d_prob * attn_prob, axis=-1, keepdims=True)]
  transfers between devices with their start and end apart: 3 -> 3, of which waited for: 3 -> 2; matrix products, arithmetic and copies ran while one was open for 0% -> 1% of each run, Pallas kernels for 0% -> 5%
where the time goes in v1:
time: 553 us; the launch traced here: 552 us
  waiting for transfers between devices  374 us (68%)
  Pallas kernels  112 us (20%)
  local copies, waits for them, and re-layouts  24.5 us (4%)
  blocking collectives  19.5 us (4%)
  between operations  14.2 us (3%)
    psum x2, waiting for transfers between devices, device_fn(): total = lax.psum(grads, ('dp', 'sp'))  374 us
    pallas_call x5, Pallas kernels, call(): pl.pallas_call(kernel, grid=grid, in_specs=in_specs, out_specs=out_specs,...  112 us
    all_to_all x1, blocking collectives, device_fn(): result = lax.all_to_all(result.reshape(cot.shape), 'sp', 0, 1, tiled=True)  19.5 us
    unnamed x59, local copies, waits for them, and re-layouts  17.7 us
  transfers between devices with their start and end apart: 3, of which 2 were waited for; matrix products, arithmetic and copies ran while one was open for 1% of the time, Pallas kernels for 5%

profile of v1, /device:TPU:0, one launch (start us, length us, event | category | flops | bytes accessed | tf_op | source)
XLA Modules:
  0.0 552.0 jit_solution(4440616232467394195)
XLA Ops:
  7.2 4.4 all-to-all-start
  11.7 0.8 copy.35
  14.8 0.6 pad_convert_fusion.table_ref
  15.4 10.8 %pos.1.pos_ref = f32[2,144,1152]{2,1,0:T(8,128)} custom-call(f32[16,640]{1,0:T(8,128)} %pad_convert_fusion.table_ref, s32[144,144]{1,0:T(8,128)} %bitcast.22), custom_call_target="tpu_custom_call" | custom-call | flops 10000000 | bytes 1451008 | tf_op jit(solution)/shard_map/pos/pallas_call | solution.py:299
  26.2 19.6 %fwd.1 = (bf16[4,288,1024]{2,1,0:T(8,128)(2,1)}, bf16[4,288,512]{2,1,0:T(8,128)(2,1)}, bf16[4,288,1536]{2,1,0:T(8,128)(2,1)}, bf16[4,288,512]{2,1,0:T(8,128)(2,1...) custom-call(bf16[4,24,48,256]{3,2,1,0:T(8,128)(2,1)} %tok_ref.1, ...), custom_call_target="tpu_custom_call" | custom-call | flops 8000000000 | bytes 16648192 | tf_op jit(solution)/shard_map/fwd/pallas_call | solution.py:299
  45.8 1.0 copy-done.5
  46.8 28.7 %mlp.1 = (bf16[4,288,512]{2,1,0:T(8,128)(2,1)}, f32[4,288,512]{2,1,0:T(8,128)}, f32[512,2048]{1,0:T(8,128)}, f32[2048,512]{1,0:T(8,128)}, f32[1,2048]{1,0:T(1,128)}, /*index=5*/f32[1,512]{1,0:T(1,128)}, f32[2,512]{1,0:T(2,128)}) custom-call(bf16[4,288,512]{2,1,0:T(8,128)(2,1)} %get-tuple-element.37.h1_ref, bf16[4,288,512]{2,1,0:T(8,128)(2,1)} %bitcast.21, ...), custom_call_target="tpu_custom_call" | custom-call | flops 16000000000 | bytes 18668544 | tf_op jit(solution)/shard_map/mlp/pallas_call | solution.py:299
  75.5 35.7 %bwd.1 = (bf16[4,24,48,256]{3,2,1,0:T(8,128)(2,1)}, f32[512,512]{1,0:T(8,128)}, f32[512,1536]{1,0:T(8,128)}, f32[1024,512]{1,0:T(8,128)}, f32[1,512]{1,0:T(1,128...) custom-call(f32[4,288,512]{2,1,0:T(8,128)} %get-tuple-element.39.dh1_ref, ...), custom_call_target="tpu_custom_call" | custom-call | flops 16000000000 | bytes 25462784 | tf_op jit(solution)/shard_map/bwd/pallas_call | solution.py:299
  111.2 2.7 reshape.70
  113.8 1.8 copy.39
  115.6 17.6 %table.1 = f32[48,640]{1,0:T(8,128)} custom-call(f32[144,16,144]{2,1,0:T(8,128)} %bitcast.18, s32[144,144]{1,0:T(8,128)} %bitcast.23), custom_call_target="tpu_custom_call" | custom-call | flops 1000000000 | bytes 1532928 | tf_op jit(solution)/shard_map/table/pallas_call | solution.py:299
  133.3 0.6 reduce
  133.9 1.5 reduce_sum.9
  135.5 0.7 all-reduce.8.cloned.1.call-update
  136.8 19.5 %all_to_all.21 = bf16[4,12,24,512]{3,2,1,0:T(8,128)(2,1)S(1)} all-to-all(bf16[4,12,24,512]{3,2,1,0:T(8,128)(2,1)S(1)} %bitcast.20), channel_id=1, replica_groups=mesh['dp'=8,'sp'=4] {'sp'}, dimensions={0} | all-to-all | bytes 2359296 | tf_op jit(solution)/shard_map/all_to_all | solution.py:390
  156.3 112.5 %all-reduce.6.cloned.1.call-done = (f32[2,1024]{1,0:T(2,128)}, f32[2,512]{1,0:T(2,128)}, f32[1536]{0:T(1024)}, f32[529,16]{0,1:T(8,128)}, f32[512]{0:T(512)}, /*...) async-done(((f32[2,1024]{1,0:T(2,128)}, f32[2,512]{1,0:T(2,128)}, f32[1536]{0:T(1024)}, f32[529,16]{0,1:T(8,128)}, f32[512]{0:T(512)}, /*index=5*/f32[2,512]{1,0:T(2,128)}, ...) | async-done | bytes 68688 | tf_op jit(solution)/shard_map/psum | solution.py:391
  268.8 261.0 %all-reduce.8.cloned.1.call-done = (f32[1024,512]{1,0:T(8,128)}, f32[512,1536]{1,0:T(8,128)}, f32[512,512]{1,0:T(8,128)}, f32[512,2048]{1,0:T(8,128)}, f32[2048,512]{1,0:T(8,128)}) async-done(((f32[1024,512]{1,0:T(8,128)}, f32[512,1536]{1,0:T(8,128)}, f32[512,512]{1,0:T(8,128)}, f32[512,2048]{1,0:T(8,128)}, f32[2048,512]{1,0:T(8,128)}), (f32[1024,512]{1,0:T(8,128)}, f32[512,1536]{1,0:T(8,128)}, ...) | async-done | bytes 14680080 | tf_op jit(solution)/shard_map/psum | solution.py:391
  529.8 1.0 copy.54
  531.8 1.3 copy.56
  533.8 1.7 copy.58
  536.7 1.0 copy.61
  538.8 2.1 copy.64
  541.6 1.0 copy-done
  542.6 2.0 copy.66
  (58 shorter events, 8.2 us)
Async XLA Ops:
  7.2 4.5 copy-start.7
  7.2 5.2 copy-start.15
  7.2 5.8 %copy-start.20 = (bf16[512]{0:T(512)(128)(2,1)S(1)}, bf16[512]{0:T(512)(128)(2,1)}, u32[]{:S(2)}) copy-start(bf16[512]{0:T(512)(128)(2,1)} %param.28) | copy-start | bytes 3076
  7.2 6.4 %copy-start.14 = (bf16[2048]{0:T(1024)(128)(2,1)S(1)}, bf16[2048]{0:T(1024)(128)(2,1)}, u32[]{:S(2)}) copy-start(bf16[2048]{0:T(1024)(128)(2,1)} %param.31) | copy-start | bytes 12292
  7.2 7.0 %copy-start.21 = (bf16[512]{0:T(512)(128)(2,1)S(1)}, bf16[512]{0:T(512)(128)(2,1)}, u32[]{:S(2)}) copy-start(bf16[512]{0:T(512)(128)(2,1)} %param.33) | copy-start | bytes 3076
  7.2 7.6 %copy-start.9 = (bf16[529,16]{0,1:T(8,128)(2,1)S(1)}, bf16[529,16]{0,1:T(8,128)(2,1)}, u32[]{:S(2)}) copy-start(bf16[529,16]{0,1:T(8,128)(2,1)} %param.26) | copy-start | bytes 50788
  7.2 38.5 %all-to-all-start = ((bf16[1,48,24,512]{3,2,0,1:T(8,128)(2,1)}), bf16[1,48,24,512]{3,2,0,1:T(8,128)(2,1)S(1)}, u32[]{:S(2)}, u32[]{:S(2)}) async-start(bf16[1,48,24,512]{3,2,0,1:T(8,128)(2,1)} %bitcast.19), calls=%async_computation | async-start | bytes 2359296 | tf_op jit(solution)/shard_map/all_to_all | solution.py:388
  11.7 257.1 %all-reduce.6.cloned.1.call-start = ((), (), s32[]{:S(2)}) async-start(), calls=%async_computation.2 | async-start | bytes 155648 | tf_op jit(solution)/shard_map/psum | solution.py:391
  115.6 17.6 %copy-start.13 = (f32[1,1536]{1,0:T(1,128)S(1)}, f32[1,1536]{1,0:T(1,128)}, u32[]{:S(2)}) copy-start(f32[1,1536]{1,0:T(1,128)} %get-tuple-element.50) | copy-start | bytes 18436
  135.5 394.3 %all-reduce.8.cloned.1.call-start = ((), (), s32[]{:S(2)}) async-start(), calls=%async_computation.3 | async-start | bytes 29360128 | tf_op jit(solution)/shard_map/psum | solution.py:391
  135.5 1.3 copy-start.4
  268.8 262.0 %copy-start.12 = (f32[2,1024]{1,0:T(2,128)S(1)}, f32[2,1024]{1,0:T(2,128)}, u32[]{:S(2)}) copy-start(f32[2,1024]{1,0:T(2,128)} %get-tuple-element.89) | copy-start | bytes 24580
  529.8 2.0 copy-start.3
  530.8 2.3 copy-start.17
  530.8 2.9 copy-start.2
  533.7 1.7 copy-start.11
  533.8 2.3 copy-start.8
  533.8 2.9 copy-start.6
  533.8 3.9 copy-start.19
  533.8 4.5 copy-start.16
  533.8 5.1 copy-start.1
  538.8 2.1 copy-start.10
  538.8 3.7 copy-start
  542.6 2.0 copy-start.18
  (1 other events, 1.0 us)
Sparse Core Ops, SparseCore 0:
  135.6 133.1 all-reduce.5
  276.3 253.4 all-reduce.7

commit v2 on v1

--- a/solution.py
+++ b/solution.py
@@ -61,6 +61,11 @@
     for h in range(1, len(masks)):
         total = total + x[h * seq:(h + 1) * seq] * masks[h]
     return total
+
+
+def pack(ref, at, value):
+    ref[at] = value[:256]
+    ref[at + 1] = value[256:]
 
 
 def pos_kernel(table_ref, idx_ref, pos_ref):
@@ -120,7 +125,7 @@
 
 
 def mlp_kernel(h1_ref, cot_ref, perm_ref, nb_ref, w1_ref, b1_ref, w2_ref, b2_ref,
-               out_ref, dh1_ref, gw1_ref, gw2_ref, gb1_ref, gb2_ref, gnb_ref,
+               out_ref, dh1_ref, gw_ref, gb1_ref, gb2_ref, gnb_ref,
                hid_s, dpre_s, b_s, cot_s):
     i = pl.program_id(0)
     n = h1_ref.shape[1]
@@ -166,14 +171,14 @@
     def _():
         def body(c, carry):
             cols = pl.ds(pl.multiple_of(c * chunk, chunk), chunk)
-            gw1_ref[:, cols] = dot_tn(b_s[...], dpre_s[:, cols])
-            gw2_ref[cols, :] = dot_tn(hid_s[:, cols], cot_s[...])
+            pack(gw_ref, 2 * c, dot_tn(b_s[...], dpre_s[:, cols]))
+            pack(gw_ref, 2 * (w1_ref.shape[1] // chunk + c), dot_tn(hid_s[:, cols], cot_s[...]))
             return carry
         lax.fori_loop(0, w1_ref.shape[1] // chunk, body, 0)
 
 
 def bwd_kernel(dh1_ref, raw_ref, h0_ref, qkv_ref, att_ref, lse_ref, perm_ref, pos_ref, nm_ref, wr_ref, na_ref, wq_ref, wp_ref,
-               gtok_ref, gwp_ref, gwq_ref, gwr_ref, gbp_ref, gbq_ref, gna_ref, gnm_ref, gpos_ref,
+               gtok_ref, gw_ref, gbp_ref, gbq_ref, gna_ref, gnm_ref, gpos_ref,
                att_s, dh1_s, a_s, dqkv_s, m_s, dh0_s, datt_s, dqkv_f, *, head_dim, seq):
     i = pl.program_id(0)
     n = dh1_ref.shape[1]
@@ -240,19 +245,21 @@
 
     @pl.when(i == pl.num_programs(0) - 1)
     def _():
-        gwp_ref[...] = dot_tn(att_s[...], dh1_s[...])
+        n_red = m_s.shape[1] // 512
+        n_qkv = dqkv_s.shape[1] // 512
+
+        def body_r(c, carry):
+            cols = pl.ds(pl.multiple_of(c * 512, 512), 512)
+            pack(gw_ref, 2 * c, dot_tn(m_s[:, cols], dh0_s[...]))
+            return carry
+        lax.fori_loop(0, n_red, body_r, 0)
 
         def body_q(c, carry):
             cols = pl.ds(pl.multiple_of(c * 512, 512), 512)
-            gwq_ref[:, cols] = dot_tn(a_s[...], dqkv_s[:, cols])
+            pack(gw_ref, 2 * (n_red + c), dot_tn(a_s[...], dqkv_s[:, cols]))
             return carry
-        lax.fori_loop(0, gwq_ref.shape[1] // 512, body_q, 0)
-
-        def body_r(c, carry):
-            cols = pl.ds(pl.multiple_of(c * 512, 512), 512)
-            gwr_ref[cols, :] = dot_tn(m_s[:, cols], dh0_s[...])
-            return carry
-        lax.fori_loop(0, gwr_ref.shape[0] // 512, body_r, 0)
+        lax.fori_loop(0, n_qkv, body_q, 0)
+        pack(gw_ref, 2 * (n_red + n_qkv), dot_tn(att_s[...], dh1_s[...]))
 
 
 def table_kernel(gpos_ref, idx_ref, out_ref, parts_s, *, n_heads):
@@ -355,17 +362,17 @@
         [band(tokens.shape)] + [whole(a.shape) for a in ins[1:]], outs, [band(o.shape) for o in outs], [], 8 * 10**9, "fwd")
 
     ins = (h1, cot.reshape(nb, n, dim), perm_w, norm_mlp, w_fc1, row(b_fc1), w_fc2, row(b_fc2))
-    outs = [sds((nb, n, dim), BF), sds((nb, n, dim), F32), sds((dim, ff), F32), sds((ff, dim), F32), sds((1, ff), F32), sds((1, dim), F32), sds((2, dim), F32)]
-    result, dh1, g_w1, g_w2, g_b1, g_b2, g_nb = call(
+    outs = [sds((nb, n, dim), BF), sds((nb, n, dim), F32), sds((4 * ff // 512, 256, 512), F32), sds((1, ff), F32), sds((1, dim), F32), sds((2, dim), F32)]
+    result, dh1, gw_mlp, g_b1, g_b2, g_nb = call(
         mlp_kernel, (nb,), ins, [band(ins[0].shape), band(ins[1].shape)] + [whole(a.shape) for a in ins[2:]],
         outs, [band(outs[0].shape), band(outs[1].shape)] + [out_whole(o.shape) for o in outs[2:]],
         [pltpu.VMEM((nb * n, ff), BF), pltpu.VMEM((nb * n, ff), BF), pltpu.VMEM((nb * n, dim), BF), pltpu.VMEM((nb * n, dim), BF)],
         16 * 10**9, "mlp")
 
     ins = (dh1, raw, h0, qkv, att, lse, perm4, pos, norm_merge, w_reduce, norm_attn, w_qkv, w_proj)
-    outs = [sds(tokens.shape, BF), sds((dim, dim), F32), sds((dim, 3 * dim), F32), sds((4 * chan, dim), F32), sds((1, dim), F32),
+    outs = [sds(tokens.shape, BF), sds((2 * (dim + 3 * dim + 4 * chan) // 512, 256, 512), F32), sds((1, dim), F32),
             sds((1, 3 * dim), F32), sds((2, dim), F32), sds((2, 4 * chan), F32), sds((groups, seq, lanes), F32)]
-    g_tok, g_wp, g_wq, g_wr, g_bp, g_bq, g_na, g_nm, g_pos = call(
+    g_tok, gw_att, g_bp, g_bq, g_na, g_nm, g_pos = call(
         functools.partial(bwd_kernel, head_dim=head_dim, seq=seq), (nb,), ins,
         [band(a.shape) for a in ins[:6]] + [whole(a.shape) for a in ins[6:]],
         outs, [band(outs[0].shape)] + [out_whole(o.shape) for o in outs[1:]],
@@ -378,18 +385,146 @@
     parts = call(functools.partial(table_kernel, n_heads=n_heads), (seq // block,), (g_pos, idx_t),
                  [pl.BlockSpec((block, n_heads, seq), lambda i: (i, 0, 0)), pl.BlockSpec((block, seq), lambda i: (i, 0))],
                  [sds((3 * n_heads, table_pad), F32)], [out_whole((3 * n_heads, table_pad))], [pltpu.VMEM((8, 128), F32)], 10**9, "table")[0]
-    g_table = parts.reshape(3, n_heads, table_pad).sum(0).T[:rel_table.shape[0]]
-    return result, g_tok, (g_nm, g_wr, g_na, g_wq, g_bq[0], g_table, g_wp, g_bp[0], g_nb, g_w1, g_b1[0], g_w2, g_b2[0])
+    g_table = parts.reshape(3, n_heads, table_pad).sum(0)
+    small = jnp.concatenate([x.reshape(-1) for x in (g_nm, g_na, g_nb, g_bq, g_bp, g_b1, g_b2, g_table)])
+    small = jnp.pad(small, (0, 256 * 128 - small.shape[0])).reshape(256, 128)
+    return result, g_tok, gw_mlp, gw_att, small
+
+
+ORDERS = (('core', 'x', 'y', 'z0', 'z1'), ('core', 'y', 'x', 'z0', 'z1'))
+HALVES = (128, 64, 32, 16, 8)
+LAND = (0, 128, 192, 224, 240)
+
+
+def place():
+    dp, sp = lax.axis_index('dp'), lax.axis_index('sp')
+    bits = {'core': sp % 2, 'x': sp // 2, 'y': dp % 2, 'z0': (dp // 2) % 2, 'z1': dp // 4}
+    unit = {'core': (0, 1), 'x': (0, 2), 'y': (1, 0), 'z0': (2, 0), 'z1': (4, 0)}
+    peers = {k: (dp + (1 - 2 * b) * unit[k][0], sp + (1 - 2 * b) * unit[k][1]) for k, b in bits.items()}
+    return bits, peers
+
+
+class Stream:
+    def __init__(self, order, ins, land, outs, send, recv):
+        bits, self.peers = place()
+        self.order, self.ins, self.land, self.outs, self.send, self.recv = order, ins, land, outs, send, recv
+        self.bits = [bits[k] for k in order]
+        offs = [0]
+        for b, half in zip(self.bits, HALVES):
+            offs.append(offs[-1] + b * half)
+        self.offs = offs
+
+    def rows(self, start, size):
+        return pl.ds(pl.multiple_of(start, 8), size)
+
+    def copy(self, k):
+        j = k if k < 5 else 9 - k
+        half = HALVES[j]
+        if k == 0:
+            src = self.ins.at[self.rows((1 - self.bits[0]) * half, half)]
+        elif k < 5:
+            src = self.land.at[self.rows(LAND[j - 1] + (1 - self.bits[j]) * half, half)]
+        else:
+            src = self.outs.at[self.rows(self.offs[j + 1], half)]
+        dst = self.land.at[pl.ds(LAND[j], half)] if k < 5 else self.outs.at[self.rows(self.offs[j + 1], half)]
+        return pltpu.make_async_remote_copy(src_ref=src, dst_ref=dst, send_sem=self.send.at[k], recv_sem=self.recv.at[k],
+                                            device_id=self.peers[self.order[j]], device_id_type=pl.DeviceIdType.MESH)
+
+    def finish(self, k):
+        self.copy(k).wait()
+        if k < 5:
+            half = HALVES[k]
+            if k == 0:
+                kept = self.ins[self.rows(self.bits[0] * half, half), :]
+            else:
+                kept = self.land[self.rows(LAND[k - 1] + self.bits[k] * half, half), :]
+            total = self.land[pl.ds(LAND[k], half), :] + kept
+            if k < 4:
+                self.land[pl.ds(LAND[k], half), :] = total
+            else:
+                self.outs[self.rows(self.offs[5], half), :] = total
+
+    def advance(self, k):
+        if k > 0:
+            self.finish(k - 1)
+        if k < 10:
+            self.copy(k).start()
+
+
+def reduce_kernel(*refs, counts):
+    n = len(counts)
+    ins, small_in = refs[:n], refs[n]
+    outs, small_out = refs[n + 1:2 * n + 1], refs[2 * n + 1]
+    land, small_land, send, recv, small_send, small_recv = refs[2 * n + 2:]
+    peers = place()[1]
+    barrier = pltpu.get_barrier_semaphore()
+    for k in ORDERS[0]:
+        pl.semaphore_signal(barrier, inc=1, device_id=peers[k], device_id_type=pl.DeviceIdType.MESH)
+    pl.semaphore_wait(barrier, 5)
+    base = 0
+    slots = sum(counts) // 2
+    groups = []
+    for ref_in, ref_out, count in zip(ins, outs, counts):
+        groups.append((base // 2, count // 2, ref_in, ref_out))
+        base += count
+
+    def tick(t, carry):
+        for k in range(10, -1, -1):
+            for first, length, ref_in, ref_out in groups:
+                @pl.when((t - k >= first) & (t - k < first + length))
+                def _():
+                    u = t - k
+                    for side in range(2):
+                        s = 2 * u + side
+                        i = s - 2 * first
+                        Stream(ORDERS[side], ref_in.at[i], land.at[s], ref_out.at[i], send.at[s], recv.at[s]).advance(k)
+
+            @pl.when(t == k)
+            def _():
+                Stream(ORDERS[0], small_in, small_land, small_out, small_send, small_recv).advance(k)
+        return carry
+    lax.fori_loop(0, slots + 10, tick, 0)
+
+
+def reduce_all(arrays, small):
+    counts = tuple(a.shape[0] for a in arrays)
+    total = sum(counts)
+    vmem = pl.BlockSpec(memory_space=pltpu.VMEM)
+    outs = [sds(a.shape, F32) for a in arrays] + [sds(small.shape, F32)]
+    return pl.pallas_call(
+        functools.partial(reduce_kernel, counts=counts), in_specs=[vmem] * (len(arrays) + 1), out_specs=[vmem] * len(outs), out_shape=outs,
+        scratch_shapes=[pltpu.VMEM((total, 248, 512), F32), pltpu.VMEM((248, 128), F32), pltpu.SemaphoreType.DMA((total, 10)),
+                        pltpu.SemaphoreType.DMA((total, 10)), pltpu.SemaphoreType.DMA((10,)), pltpu.SemaphoreType.DMA((10,))],
+        name="reduce", compiler_params=pltpu.CompilerParams(collective_id=0, has_side_effects=True, vmem_limit_bytes=VMEM_LIMIT))(*arrays, small)
+
+
+def unpack(gw_mlp, gw_att, small, shapes):
+    (s_nm, s_wr, s_na, s_wq, s_bq, s_table, s_wp, s_bp, s_nb, s_w1, s_b1, s_w2, s_b2) = shapes
+    flat = small.reshape(-1)
+    got, at = [], 0
+    for shape in (s_nm, s_na, s_nb, s_bq, s_bp, s_b1, s_b2):
+        size = math.prod(shape)
+        got.append(flat[at:at + size].reshape(shape))
+        at += size
+    g_nm, g_na, g_nb, g_bq, g_bp, g_b1, g_b2 = got
+    pad = -(-s_table[0] // 128) * 128
+    g_table = flat[at:at + s_table[1] * pad].reshape(s_table[1], pad).T[:s_table[0]]
+    wide = lambda x, shape: x.reshape(-1, shape[0], 512).transpose(1, 0, 2).reshape(shape)
+    n1 = s_w1[1] // 256
+    g_w1, g_w2 = wide(gw_mlp[:n1], s_w1), gw_mlp[n1:].reshape(s_w2)
+    nr, nq = s_wr[0] // 256, s_wq[1] // 256
+    g_wr, g_wq, g_wp = gw_att[:nr].reshape(s_wr), wide(gw_att[nr:nr + nq], s_wq), gw_att[nr + nq:].reshape(s_wp)
+    return g_nm, g_wr, g_na, g_wq, g_bq, g_table, g_wp, g_bp, g_nb, g_w1, g_b1, g_w2, g_b2
 
 
 def solution(mesh):
     def device_fn(tokens, grad_out, rel_index, *weights):
         nb = mesh.shape['sp']
         cot = lax.all_to_all(grad_out, 'sp', 1, 0, tiled=True)
-        result, g_tok, grads = local_step(tokens, cot, rel_index, weights)
+        result, g_tok, gw_mlp, gw_att, small = local_step(tokens, cot, rel_index, weights)
         result = lax.all_to_all(result.reshape(cot.shape), 'sp', 0, 1, tiled=True)
-        total = lax.psum(grads, ('dp', 'sp'))
-        return (result, g_tok) + tuple(total)
+        gw_mlp, gw_att, small = reduce_all([gw_mlp, gw_att], small)
+        return (result, g_tok) + unpack(gw_mlp, gw_att, small, [w.shape for w in weights])
 
     rep_specs = (P(),) * 13
     return jax.shard_map(device_fn, mesh=mesh, in_specs=(P('dp', 'sp'), P(('dp', 'sp')), P()) + rep_specs, out_specs=(P(('dp', 'sp')), P('dp', 'sp')) + rep_specs, check_vma=False)

time: 553 us -> 328 us (0.59)
  waiting for transfers between devices: 374 us -> 0.01 us
  Pallas kernels: 112 us -> 276 us
  blocking collectives: 19.5 us -> 0 us
  local copies, waits for them, and re-layouts: 24.5 us -> 40.5 us
  between operations: 14.2 us -> 0.88 us
    psum x2 -> x0, waiting for transfers between devices: 374 us -> none  [device_fn(): total = lax.psum(grads, ('dp', 'sp'))]
    pallas_call x0 -> x1, Pallas kernels: none -> 164 us  [reduce_all(): pl.pallas_call(functools.partial(reduce_kernel, counts=counts), in_specs=...]
    all_to_all x1 -> x0, blocking collectives: 19.5 us -> none  [device_fn(): result = lax.all_to_all(result.reshape(cot.shape), 'sp', 0, 1, tiled=True)]
    slice x0 -> x9, local copies, waits for them, and re-layouts: none -> 15.8 us  [the longest x1 6.51 us: unpack(): g_w1, g_w2 = (wide(gw_mlp[:n1], s_w1), gw_mlp[n1:].reshape(s_w2))]
    reshape x0 -> x8, local copies, waits for them, and re-layouts: none -> 7.93 us  [the longest x2 4.83 us: unpack(): x.reshape(-1, shape[0], 512).transpose(1, 0, 2).reshape(shape)]
    unnamed x59 -> x36, local copies, waits for them, and re-layouts: 17.7 us -> 9.92 us
  transfers between devices with their start and end apart: 3 -> 2, of which waited for: 2 -> 0; matrix products, arithmetic and copies ran while one was open for 1% -> 7% of each run, Pallas kernels for 5% -> 9%
where the time goes in v2:
time: 328 us
  Pallas kernels  276 us (84%)
  local copies, waits for them, and re-layouts  40.5 us (12%)
  starting transfers between devices  8.7 us (3%)
    pallas_call x1, Pallas kernels, reduce_all(): pl.pallas_call(functools.partial(reduce_kernel, counts=counts), in_specs=...  164 us
    pallas_call x5, Pallas kernels, call(): pl.pallas_call(kernel, grid=grid, in_specs=in_specs, out_specs=out_specs,...  112 us
    unnamed x36, local copies, waits for them, and re-layouts  9.92 us
  transfers between devices with their start and end apart: 2, of which 0 were waited for; matrix products, arithmetic and copies ran while one was open for 7% of the time, Pallas kernels for 9%

profile of v2, /device:TPU:0, one launch (start us, length us, event | category | flops | bytes accessed | tf_op | source)
XLA Modules:
  0.0 327.6 jit_solution(10928104598353800014)
XLA Ops:
  0.7 4.4 %all-to-all-start = ((bf16[1,48,24,512]{3,2,0,1:T(8,128)(2,1)}), bf16[1,48,24,512]{3,2,0,1:T(8,128)(2,1)S(1)}, u32[]{:S(2)}, u32[]{:S(2)}) async-start(bf16[1,48,24,512]{3,2,0,1:T(8,128)(2,1)} %bitcast.53), calls=%async_computation | async-start | bytes 2359296 | tf_op jit(solution)/shard_map/all_to_all | solution.py:523
  7.5 0.8 copy.42
  8.9 10.7 %pos.1.pos_ref = f32[2,144,1152]{2,1,0:T(8,128)} custom-call(f32[16,640]{1,0:T(8,128)} %pad_convert_fusion.table_ref, s32[144,144]{1,0:T(8,128)} %bitcast.57), custom_call_target="tpu_custom_call" | custom-call | flops 10000000 | bytes 1451008 | tf_op jit(solution)/shard_map/pos/pallas_call | solution.py:306
  19.6 19.4 %fwd.1 = (bf16[4,288,1024]{2,1,0:T(8,128)(2,1)}, bf16[4,288,512]{2,1,0:T(8,128)(2,1)}, bf16[4,288,1536]{2,1,0:T(8,128)(2,1)}, bf16[4,288,512]{2,1,0:T(8,128)(2,1...) custom-call(bf16[4,24,48,256]{3,2,1,0:T(8,128)(2,1)} %tok_ref.1, ...), custom_call_target="tpu_custom_call" | custom-call | flops 8000000000 | bytes 16648192 | tf_op jit(solution)/shard_map/fwd/pallas_call | solution.py:306
  39.0 1.1 copy-done
  40.1 28.8 %mlp.1 = (bf16[4,288,512]{2,1,0:T(8,128)(2,1)}, f32[4,288,512]{2,1,0:T(8,128)}, f32[16,256,512]{2,1,0:T(8,128)}, f32[1,2048]{1,0:T(1,128)}, f32[1,512]{1,0:T(1,128)}, /*index=5*/f32[2,512]{1,0:T(2,128)}) custom-call(bf16[4,288,512]{2,1,0:T(8,128)(2,1)} %get-tuple-element.37.h1_ref, bf16[4,288,512]{2,1,0:T(8,128)(2,1)} %bitcast.55, ...), custom_call_target="tpu_custom_call" | custom-call | flops 16000000000 | bytes 18668544 | tf_op jit(solution)/shard_map/mlp/pallas_call | solution.py:306
  68.9 0.7 copy.51
  69.6 35.6 %bwd.1 = (bf16[4,24,48,256]{3,2,1,0:T(8,128)(2,1)}, f32[12,256,512]{2,1,0:T(8,128)}, f32[1,512]{1,0:T(1,128)}, f32[1,1536]{1,0:T(1,128)}, f32[2,512]{1,0:T(2,128...) custom-call(f32[4,288,512]{2,1,0:T(8,128)} %get-tuple-element.39.dh1_ref, ...), custom_call_target="tpu_custom_call" | custom-call | flops 16000000000 | bytes 25462784 | tf_op jit(solution)/shard_map/bwd/pallas_call | solution.py:306
  105.2 0.7 copy.50
  105.9 0.7 bitcast_dynamic-update-slice_fusion
  106.6 2.7 reshape.150
  109.3 1.8 copy.54
  111.0 17.7 %table.1 = f32[48,640]{1,0:T(8,128)} custom-call(f32[144,16,144]{2,1,0:T(8,128)} %bitcast.51, s32[144,144]{1,0:T(8,128)} %bitcast.58), custom_call_target="tpu_custom_call" | custom-call | flops 1000000000 | bytes 1532928 | tf_op jit(solution)/shard_map/table/pallas_call | solution.py:306
  128.7 0.9 reduce_sum.9
  130.5 163.7 %reduce.2 = (f32[16,256,512]{2,1,0:T(8,128)}, f32[12,256,512]{2,1,0:T(8,128)}, f32[256,128]{1,0:T(8,128)}) custom-call(f32[16,256,512]{2,1,0:T(8,128)} %get-tuple-element.46.refs_0_, f32[12,256,512]{2,1,0:T(8,128)} %get-tuple-element.47.refs_1_, f32[256,128]{1,0:T(8,128)} %pad_bitcast_fusion.refs_2_), custom_call_target="tpu_custom_call" | custom-call | tf_op jit(solution)/shard_map/reduce/pallas_call | solution.py:494
  294.2 2.3 slice.66
  296.5 3.1 slice.59
  299.6 2.2 slice.61
  301.8 4.3 %all-to-all-start.1 = ((bf16[4,12,24,512]{3,2,1,0:T(8,128)(2,1)}), bf16[4,12,24,512]{3,2,1,0:T(8,128)(2,1)}, u32[]{:S(2)}, u32[]{:S(2)}) async-start(bf16[4,12,24,512]{3,2,1,0:T(8,128)(2,1)} %bitcast.54), calls=%async_computation.1 | async-start | bytes 2359296 | tf_op jit(solution)/shard_map/all_to_all | solution.py:525
  306.1 6.5 %fusion = (f32[8,256,512]{2,1,0:T(8,128)}, f32[8,256,512]{2,1,0:T(8,128)S(1)}) fusion(f32[16,256,512]{2,1,0:T(8,128)} %get-tuple-element.58), kind=kLoop, calls=%fused_computation.15 | loop fusion | bytes 16777216 | tf_op jit(solution)/shard_map/slice | solution.py:514
  312.6 2.5 copy.48
  318.1 2.3 copy.45
  320.5 3.5 %copy.47 = f32[512,1536]{1,0:T(8,128)} copy(f32[512,1536]{0,1:T(8,128)} %bitcast.48) | data formatting | bytes 6291456
  325.2 2.4 copy.63
  (49 shorter events, 8.0 us)
Async XLA Ops:
  0.6 4.5 %copy-start.10 = (bf16[512]{0:T(512)(128)(2,1)S(1)}, bf16[512]{0:T(512)(128)(2,1)}, u32[]{:S(2)}) copy-start(bf16[512]{0:T(512)(128)(2,1)} %param.28) | copy-start | bytes 3076
  0.7 5.0 %copy-start.11 = (bf16[512]{0:T(512)(128)(2,1)S(1)}, bf16[512]{0:T(512)(128)(2,1)}, u32[]{:S(2)}) copy-start(bf16[512]{0:T(512)(128)(2,1)} %param.33) | copy-start | bytes 3076
  0.7 5.6 %copy-start.7 = (bf16[1536]{0:T(1024)(128)(2,1)S(1)}, bf16[1536]{0:T(1024)(128)(2,1)}, u32[]{:S(2)}) copy-start(bf16[1536]{0:T(1024)(128)(2,1)} %param.25) | copy-start | bytes 9220
  0.7 6.2 %copy-start.6 = (bf16[2048]{0:T(1024)(128)(2,1)S(1)}, bf16[2048]{0:T(1024)(128)(2,1)}, u32[]{:S(2)}) copy-start(bf16[2048]{0:T(1024)(128)(2,1)} %param.31) | copy-start | bytes 12292
  0.7 6.8 %copy-start.1 = (s32[144,144]{1,0:T(8,128)S(1)}, s32[144,144]{1,0:T(8,128)}, u32[]{:S(2)}) copy-start(s32[144,144]{1,0:T(8,128)} %param.20) | copy-start | bytes 248836
  0.7 7.6 %copy-start.3 = (bf16[529,16]{0,1:T(8,128)(2,1)S(1)}, bf16[529,16]{0,1:T(8,128)(2,1)}, u32[]{:S(2)}) copy-start(bf16[529,16]{0,1:T(8,128)(2,1)} %param.26) | copy-start | bytes 50788
  0.7 38.2 %all-to-all-start = ((bf16[1,48,24,512]{3,2,0,1:T(8,128)(2,1)}), bf16[1,48,24,512]{3,2,0,1:T(8,128)(2,1)S(1)}, u32[]{:S(2)}, u32[]{:S(2)}) async-start(bf16[1,48,24,512]{3,2,0,1:T(8,128)(2,1)} %bitcast.53), calls=%async_computation | async-start | bytes 2359296 | tf_op jit(solution)/shard_map/all_to_all | solution.py:523
  39.0 1.1 copy-start
  111.0 18.6 %copy-start.5 = (f32[1,1536]{1,0:T(1,128)S(1)}, f32[1,1536]{1,0:T(1,128)}, u32[]{:S(2)}) copy-start(f32[1,1536]{1,0:T(1,128)} %get-tuple-element.51) | copy-start | bytes 18436
  111.0 18.7 %copy-start.9 = (f32[1,512]{1,0:T(1,128)S(1)}, f32[1,512]{1,0:T(1,128)}, u32[]{:S(2)}) copy-start(f32[1,512]{1,0:T(1,128)} %get-tuple-element.52) | copy-start | bytes 6148
  111.0 18.7 %copy-start.4 = (f32[1,2048]{1,0:T(1,128)S(1)}, f32[1,2048]{1,0:T(1,128)}, u32[]{:S(2)}) copy-start(f32[1,2048]{1,0:T(1,128)} %get-tuple-element.53) | copy-start | bytes 24580
  111.0 18.7 %copy-start.8 = (f32[1,512]{1,0:T(1,128)S(1)}, f32[1,512]{1,0:T(1,128)}, u32[]{:S(2)}) copy-start(f32[1,512]{1,0:T(1,128)} %get-tuple-element.54) | copy-start | bytes 6148
  301.8 23.4 %all-to-all-start.1 = ((bf16[4,12,24,512]{3,2,1,0:T(8,128)(2,1)}), bf16[4,12,24,512]{3,2,1,0:T(8,128)(2,1)}, u32[]{:S(2)}, u32[]{:S(2)}) async-start(bf16[4,12,24,512]{3,2,1,0:T(8,128)(2,1)} %bitcast.54), calls=%async_computation.1 | async-start | bytes 2359296 | tf_op jit(solution)/shard_map/all_to_all | solution.py:525
  312.6 2.5 copy-start.2

commit v3 on v1

--- a/solution.py
+++ b/solution.py
@@ -120,10 +120,8 @@
 
 
 def mlp_kernel(h1_ref, cot_ref, perm_ref, nb_ref, w1_ref, b1_ref, w2_ref, b2_ref,
-               out_ref, dh1_ref, gw1_ref, gw2_ref, gb1_ref, gb2_ref, gnb_ref,
-               hid_s, dpre_s, b_s, cot_s):
+               out_ref, dh1_ref, hid_ref, dpre_ref, b_ref, cotw_ref, gb1_ref, gb2_ref, gnb_ref):
     i = pl.program_id(0)
-    n = h1_ref.shape[1]
 
     @pl.when(i == 0)
     def _():
@@ -131,14 +129,13 @@
         gb2_ref[...] = jnp.zeros(gb2_ref.shape, F32)
         gnb_ref[...] = jnp.zeros(gnb_ref.shape, F32)
 
-    rows = pl.ds(pl.multiple_of(i * n, n), n)
     h1 = h1_ref[0].astype(F32)
     normed, hat, rstd = norm_fwd(h1, nb_ref)
     nb = normed.astype(BF)
-    b_s[rows, :] = nb
+    b_ref[0] = nb
     cot = dot_nn(perm_ref[...], cot_ref[0])
     cot_bf = cot.astype(BF)
-    cot_s[rows, :] = cot_bf
+    cotw_ref[0] = cot_bf
     gb2_ref[...] += jnp.sum(cot, axis=0, keepdims=True)
     out = h1 + b2_ref[...].astype(F32)
     d_norm = jnp.zeros(h1.shape, F32)
@@ -148,13 +145,13 @@
         pre = dot_nn(nb, w1_ref[:, cols]) + b1_ref[:, cols].astype(F32)
         phi = 0.5 + 0.5 * lax.erf(pre * math.sqrt(0.5))
         hid = (pre * phi).astype(BF)
-        hid_s[rows, cols] = hid
+        hid_ref[0, :, cols] = hid
         out = out + dot_nn(hid, w2_ref[cols, :])
         d_act = phi + pre * (jnp.exp(pre * pre * -0.5) * (1.0 / math.sqrt(2.0 * math.pi)))
         d_pre = dot_nt(cot_bf, w2_ref[cols, :]) * d_act
         gb1_ref[:, cols] += jnp.sum(d_pre, axis=0, keepdims=True)
         d_pre_bf = d_pre.astype(BF)
-        dpre_s[rows, cols] = d_pre_bf
+        dpre_ref[0, :, cols] = d_pre_bf
         d_norm = d_norm + dot_nt(d_pre_bf, w1_ref[:, cols])
     out_ref[0] = dot_tn(perm_ref[...], out.astype(BF)).astype(BF)
     dx, g_gain, g_shift = norm_bwd(d_norm, hat, rstd, nb_ref)
@@ -162,21 +159,11 @@
     gnb_ref[1:2, :] += g_shift
     dh1_ref[0] = cot + dx
 
-    @pl.when(i == pl.num_programs(0) - 1)
-    def _():
-        def body(c, carry):
-            cols = pl.ds(pl.multiple_of(c * chunk, chunk), chunk)
-            gw1_ref[:, cols] = dot_tn(b_s[...], dpre_s[:, cols])
-            gw2_ref[cols, :] = dot_tn(hid_s[:, cols], cot_s[...])
-            return carry
-        lax.fori_loop(0, w1_ref.shape[1] // chunk, body, 0)
-
-
-def bwd_kernel(dh1_ref, raw_ref, h0_ref, qkv_ref, att_ref, lse_ref, perm_ref, pos_ref, nm_ref, wr_ref, na_ref, wq_ref, wp_ref,
-               gtok_ref, gwp_ref, gwq_ref, gwr_ref, gbp_ref, gbq_ref, gna_ref, gnm_ref, gpos_ref,
-               att_s, dh1_s, a_s, dqkv_s, m_s, dh0_s, datt_s, dqkv_f, *, head_dim, seq):
+
+def bwd_kernel(dh1_ref, raw_ref, h0_ref, qkv_ref, lse_ref, perm_ref, pos_ref, nm_ref, wr_ref, na_ref, wq_ref, wp_ref,
+               gtok_ref, dh1b_ref, a_ref, dqkv_ref, m_ref, dh0_ref, gbp_ref, gbq_ref, gna_ref, gnm_ref, gpos_ref,
+               datt_s, dqkv_f, *, head_dim, seq):
     i = pl.program_id(0)
-    n = dh1_ref.shape[1]
     dim = h0_ref.shape[2]
 
     @pl.when(i == 0)
@@ -184,12 +171,10 @@
         for ref in (gbp_ref, gbq_ref, gna_ref, gnm_ref, gpos_ref):
             ref[...] = jnp.zeros(ref.shape, F32)
 
-    here = pl.ds(pl.multiple_of(i * n, n), n)
     dh1 = dh1_ref[0]
     gbp_ref[...] += jnp.sum(dh1, axis=0, keepdims=True)
     dh1_bf = dh1.astype(BF)
-    dh1_s[here, :] = dh1_bf
-    att_s[here, :] = att_ref[0]
+    dh1b_ref[0] = dh1_bf
     datt_s[...] = dot_nt(dh1_bf, wp_ref[...]).astype(BF)
     width = HEAD_GROUP * head_dim
     masks, masks_f = head_masks(width, head_dim, BF), head_masks(width, head_dim, F32)
@@ -212,18 +197,18 @@
             dqkv_f[rows, cols[0]] = unstack_heads(dot_tn(ds_bf, k), masks_f, seq)
     gbq_ref[...] += jnp.sum(dqkv_f[...], axis=0, keepdims=True)
     dqkv_bf = dqkv_f[...].astype(BF)
-    dqkv_s[here, :] = dqkv_bf
+    dqkv_ref[0] = dqkv_bf
     d_a = dot_nt(dqkv_bf, wq_ref[...])
     normed, hat, rstd = norm_fwd(h0_ref[0].astype(F32), na_ref)
-    a_s[here, :] = normed.astype(BF)
+    a_ref[0] = normed.astype(BF)
     dx, g_gain, g_shift = norm_bwd(d_a, hat, rstd, na_ref)
     gna_ref[0:1, :] += g_gain
     gna_ref[1:2, :] += g_shift
     dh0_bf = (dh1 + dx).astype(BF)
-    dh0_s[here, :] = dh0_bf
+    dh0_ref[0] = dh0_bf
     d_m = dot_nt(dh0_bf, wr_ref[...])
     normed, hat, rstd = norm_fwd(raw_ref[0].astype(F32), nm_ref)
-    m_s[here, :] = normed.astype(BF)
+    m_ref[0] = normed.astype(BF)
     dx, g_gain, g_shift = norm_bwd(d_m, hat, rstd, nm_ref)
     gnm_ref[0:1, :] += g_gain
     gnm_ref[1:2, :] += g_shift
@@ -237,42 +222,6 @@
         y = jnp.concatenate([d_raw[w * seq + g * piece:w * seq + (g + 1) * piece, p * chan:(p + 1) * chan]
                              for p in range(4) for w in range(2)], axis=0)
         gtok_ref[0, g * tok_rows:(g + 1) * tok_rows] = dot_tn(perm_ref[...], y).astype(BF).reshape(tok_rows, gtok_ref.shape[2], chan)
-
-    @pl.when(i == pl.num_programs(0) - 1)
-    def _():
-        gwp_ref[...] = dot_tn(att_s[...], dh1_s[...])
-
-        def body_q(c, carry):
-            cols = pl.ds(pl.multiple_of(c * 512, 512), 512)
-            gwq_ref[:, cols] = dot_tn(a_s[...], dqkv_s[:, cols])
-            return carry
-        lax.fori_loop(0, gwq_ref.shape[1] // 512, body_q, 0)
-
-        def body_r(c, carry):
-            cols = pl.ds(pl.multiple_of(c * 512, 512), 512)
-            gwr_ref[cols, :] = dot_tn(m_s[:, cols], dh0_s[...])
-            return carry
-        lax.fori_loop(0, gwr_ref.shape[0] // 512, body_r, 0)
-
-
-def table_kernel(gpos_ref, idx_ref, out_ref, parts_s, *, n_heads):
-    m0 = pl.program_id(0)
-    count = idx_ref.shape[0]
-
-    @pl.when(m0 == 0)
-    def _():
-        out_ref[...] = jnp.zeros(out_ref.shape, F32)
-    acc = jnp.zeros(out_ref.shape, F32)
-    row = lax.broadcasted_iota(jnp.int32, (out_ref.shape[1], idx_ref.shape[1]), 0)
-    for j in range(count):
-        hot = jnp.where(row == idx_ref[j:j + 1, :], 1.0, 0.0).astype(BF)
-        val = gpos_ref[j]
-        hi = val.astype(BF)
-        rest = val - hi.astype(F32)
-        mid = rest.astype(BF)
-        low = (rest - mid.astype(F32)).astype(BF)
-        acc = acc + dot_nt(jnp.concatenate([hi, mid, low], axis=0), hot)
-    out_ref[...] += acc
 
 
 def whole(shape):
@@ -355,41 +304,245 @@
         [band(tokens.shape)] + [whole(a.shape) for a in ins[1:]], outs, [band(o.shape) for o in outs], [], 8 * 10**9, "fwd")
 
     ins = (h1, cot.reshape(nb, n, dim), perm_w, norm_mlp, w_fc1, row(b_fc1), w_fc2, row(b_fc2))
-    outs = [sds((nb, n, dim), BF), sds((nb, n, dim), F32), sds((dim, ff), F32), sds((ff, dim), F32), sds((1, ff), F32), sds((1, dim), F32), sds((2, dim), F32)]
-    result, dh1, g_w1, g_w2, g_b1, g_b2, g_nb = call(
+    tok = lambda width, dtype=BF: sds((nb, n, width), dtype)
+    outs = [tok(dim), tok(dim, F32), tok(ff), tok(ff), tok(dim), tok(dim), sds((1, ff), F32), sds((1, dim), F32), sds((2, dim), F32)]
+    result, dh1, hid, dpre, b_in, cot_w, g_b1, g_b2, g_nb = call(
         mlp_kernel, (nb,), ins, [band(ins[0].shape), band(ins[1].shape)] + [whole(a.shape) for a in ins[2:]],
-        outs, [band(outs[0].shape), band(outs[1].shape)] + [out_whole(o.shape) for o in outs[2:]],
-        [pltpu.VMEM((nb * n, ff), BF), pltpu.VMEM((nb * n, ff), BF), pltpu.VMEM((nb * n, dim), BF), pltpu.VMEM((nb * n, dim), BF)],
-        16 * 10**9, "mlp")
-
-    ins = (dh1, raw, h0, qkv, att, lse, perm4, pos, norm_merge, w_reduce, norm_attn, w_qkv, w_proj)
-    outs = [sds(tokens.shape, BF), sds((dim, dim), F32), sds((dim, 3 * dim), F32), sds((4 * chan, dim), F32), sds((1, dim), F32),
+        outs, [band(o.shape) for o in outs[:6]] + [out_whole(o.shape) for o in outs[6:]], [], 12 * 10**9, "mlp")
+
+    ins = (dh1, raw, h0, qkv, lse, perm4, pos, norm_merge, w_reduce, norm_attn, w_qkv, w_proj)
+    outs = [sds(tokens.shape, BF), tok(dim), tok(dim), tok(3 * dim), tok(4 * chan), tok(dim), sds((1, dim), F32),
             sds((1, 3 * dim), F32), sds((2, dim), F32), sds((2, 4 * chan), F32), sds((groups, seq, lanes), F32)]
-    g_tok, g_wp, g_wq, g_wr, g_bp, g_bq, g_na, g_nm, g_pos = call(
+    g_tok, dh1_bf, a_in, dqkv, m_in, dh0, g_bp, g_bq, g_na, g_nm, g_pos = call(
         functools.partial(bwd_kernel, head_dim=head_dim, seq=seq), (nb,), ins,
-        [band(a.shape) for a in ins[:6]] + [whole(a.shape) for a in ins[6:]],
-        outs, [band(outs[0].shape)] + [out_whole(o.shape) for o in outs[1:]],
-        [pltpu.VMEM((nb * n, dim), BF), pltpu.VMEM((nb * n, dim), BF), pltpu.VMEM((nb * n, dim), BF), pltpu.VMEM((nb * n, 3 * dim), BF),
-         pltpu.VMEM((nb * n, 4 * chan), BF), pltpu.VMEM((nb * n, dim), BF), pltpu.VMEM((n, dim), BF), pltpu.VMEM((n, 3 * dim), F32)],
-        16 * 10**9, "bwd")
-
-    g_pos = g_pos.reshape(groups, seq, HEAD_GROUP, seq).transpose(1, 0, 2, 3).reshape(seq, n_heads, seq)
-    block = 8
-    parts = call(functools.partial(table_kernel, n_heads=n_heads), (seq // block,), (g_pos, idx_t),
-                 [pl.BlockSpec((block, n_heads, seq), lambda i: (i, 0, 0)), pl.BlockSpec((block, seq), lambda i: (i, 0))],
-                 [sds((3 * n_heads, table_pad), F32)], [out_whole((3 * n_heads, table_pad))], [pltpu.VMEM((8, 128), F32)], 10**9, "table")[0]
-    g_table = parts.reshape(3, n_heads, table_pad).sum(0).T[:rel_table.shape[0]]
-    return result, g_tok, (g_nm, g_wr, g_na, g_wq, g_bq[0], g_table, g_wp, g_bp[0], g_nb, g_w1, g_b1[0], g_w2, g_b2[0])
+        [band(a.shape) for a in ins[:5]] + [whole(a.shape) for a in ins[5:]],
+        outs, [band(o.shape) for o in outs[:6]] + [out_whole(o.shape) for o in outs[6:]],
+        [pltpu.VMEM((n, dim), BF), pltpu.VMEM((n, 3 * dim), F32)], 12 * 10**9, "bwd")
+
+    small = jnp.concatenate([x.reshape(-1) for x in (g_nm, g_na, g_nb, g_bq, g_bp, g_b1, g_b2)])
+    room = 256 - n_heads * table_pad // 128
+    small = jnp.pad(small, (0, room * 128 - small.shape[0])).reshape(room, 128)
+    pairs = [(hid, cot_w), (b_in, dpre), (m_in, dh0), (a_in, dqkv), (att, dh1_bf)]
+    return result, g_tok, [tuple(x.reshape(nb * n, -1) for x in pair) for pair in pairs], small, g_pos, idx_t
+
+
+ORDERS = (('core', 'x', 'y', 'z0', 'z1'), ('core', 'y', 'x', 'z0', 'z1'), ('core', 'z0', 'z1', 'x', 'y'), ('core', 'z0', 'z1', 'y', 'x'))
+HALVES = (128, 64, 32, 16, 8)
+LAND = (0, 128, 192, 224, 240)
+WIDTH = 512
+STARTS = tuple(range(1, 23, 2))
+Z_FIRST = 5
+TABLE_STEP = 8
+
+
+def place():
+    dp, sp = lax.axis_index('dp'), lax.axis_index('sp')
+    bits = {'core': sp % 2, 'x': sp // 2, 'y': dp % 2, 'z0': (dp // 2) % 2, 'z1': dp // 4}
+    unit = {'core': (0, 1), 'x': (0, 2), 'y': (1, 0), 'z0': (2, 0), 'z1': (4, 0)}
+    peers = {k: (dp + (1 - 2 * b) * unit[k][0], sp + (1 - 2 * b) * unit[k][1]) for k, b in bits.items()}
+    return bits, peers
+
+
+class Stream:
+    def __init__(self, order, other, swap, buf, land, send, recv):
+        bits, peers = place()
+        pick = lambda a, b: a if a is b else jnp.where(swap, b, a)
+        self.buf, self.land, self.send, self.recv = buf, land, send, recv
+        self.bits = [pick(bits[a], bits[b]) for a, b in zip(order, other)]
+        self.peers = [tuple(pick(p, q) for p, q in zip(peers[a], peers[b])) for a, b in zip(order, other)]
+        offs = [0]
+        for b, half in zip(self.bits, HALVES):
+            offs.append(offs[-1] + b * half)
+        self.offs = offs
+
+    def rows(self, start, size):
+        return pl.ds(pl.multiple_of(start, 8), size)
+
+    def copy(self, k):
+        j = k if k < 5 else 9 - k
+        half = HALVES[j]
+        if k == 0:
+            src = self.buf.at[self.rows((1 - self.bits[0]) * half, half)]
+        elif k < 5:
+            src = self.land.at[self.rows(LAND[j - 1] + (1 - self.bits[j]) * half, half)]
+        else:
+            src = self.buf.at[self.rows(self.offs[j + 1], half)]
+        dst = self.land.at[pl.ds(LAND[j], half)] if k < 5 else self.buf.at[self.rows(self.offs[j + 1], half)]
+        return pltpu.make_async_remote_copy(src_ref=src, dst_ref=dst, send_sem=self.send.at[k], recv_sem=self.recv.at[k],
+                                            device_id=self.peers[j], device_id_type=pl.DeviceIdType.MESH)
+
+    def finish(self, k):
+        self.copy(k).wait()
+        if k < 5:
+            half = HALVES[k]
+            if k == 0:
+                kept = self.buf[self.rows(self.bits[0] * half, half), :]
+            else:
+                kept = self.land[self.rows(LAND[k - 1] + self.bits[k] * half, half), :]
+            total = self.land[pl.ds(LAND[k], half), :] + kept
+            if k < 4:
+                self.land[pl.ds(LAND[k], half), :] = total
+            else:
+                self.buf[self.rows(self.offs[5], half), :] = total
+
+    def advance(self, k):
+        if k > 0:
+            self.finish(k - 1)
+        if k < 10:
+            self.copy(k).start()
+
+
+def add_table(pos_s, idx_ref, table_s, first):
+    row = lax.broadcasted_iota(jnp.int32, (table_s.shape[1], idx_ref.shape[1]), 0)
+    acc = table_s[...]
+    for j in range(TABLE_STEP):
+        m = first + j
+        hot = jnp.where(row == idx_ref[pl.ds(m, 1), :], 1.0, 0.0).astype(BF)
+        val = pos_s[m]
+        hi = val.astype(BF)
+        rest = val - hi.astype(F32)
+        mid = rest.astype(BF)
+        low = (rest - mid.astype(F32)).astype(BF)
+        acc = acc + dot_nt(jnp.concatenate([hi, mid, low], axis=0), hot)
+    table_s[...] = acc
+
+
+def reduce_kernel(*refs, n):
+    pairs, (small_in, gpos_ref, idx_ref) = refs[:2 * n], refs[2 * n:2 * n + 3]
+    outs, small_out = refs[2 * n + 3:3 * n + 3], refs[3 * n + 3]
+    held = refs[3 * n + 4:5 * n + 4]
+    buf, land, small_land, pos_s, table_s, send, recv, small_send, small_recv, sem_in, sem_out = refs[5 * n + 4:]
+    seq = idx_ref.shape[0]
+    n_heads = pos_s.shape[1]
+    total = buf.shape[0]
+    loads = [pltpu.make_async_copy(a, b, sem_in.at[i]) for i, (a, b) in enumerate(zip(pairs, held))]
+    for load in loads:
+        load.start()
+    groups, base = [], 0
+    for i, out in enumerate(outs):
+        count = out.shape[0] * out.shape[1] // (512 * WIDTH)
+        groups.append((base, count, held[2 * i], held[2 * i + 1], out, loads[2 * i:2 * i + 2]))
+        base += count
+
+    def block(out, j, side):
+        wide = out.shape[1] // WIDTH
+        row0, col0 = j // wide * 512 + side * 256, j % wide * WIDTH
+        return out.at[pl.ds(pl.multiple_of(row0, 256), 256), pl.ds(pl.multiple_of(col0, WIDTH), WIDTH)]
+
+    def part(ref, j):
+        return ref[...] if ref.shape[1] == WIDTH else ref[:, pl.ds(pl.multiple_of(j * WIDTH, WIDTH), WIDTH)]
+
+    peers = place()[1]
+    barrier = pltpu.get_barrier_semaphore()
+    for k in ORDERS[0]:
+        pl.semaphore_signal(barrier, inc=1, device_id=peers[k], device_id_type=pl.DeviceIdType.MESH)
+    pl.semaphore_wait(barrier, 5)
+    table_s[...] = jnp.zeros(table_s.shape, F32)
+    room = small_in.shape[0]
+    small_out[0:room, :] = small_in[...]
+    table_ticks = seq // TABLE_STEP
+    small_at = table_ticks + 2
+    slots = total // 2
+
+    def tick(t, carry):
+        for k in range(10, -1, -1):
+            u = t - STARTS[k]
+
+            @pl.when((u >= 0) & (u < slots))
+            def _():
+                swap = lax.rem(u, Z_FIRST) == Z_FIRST - 1
+                for side in range(2):
+                    s = 2 * u + side
+                    Stream(ORDERS[side], ORDERS[2 + side], swap, buf.at[s], land.at[s], send.at[s], recv.at[s]).advance(k)
+                if k == 10:
+                    for first, count, left, right, out, loads in groups:
+                        @pl.when((u >= first) & (u < first + count))
+                        def _():
+                            for side in range(2):
+                                s = 2 * u + side
+                                pltpu.make_async_copy(buf.at[s], block(out, u - first, side), sem_out.at[s]).start()
+
+            @pl.when(t == small_at + k)
+            def _():
+                Stream(ORDERS[0], ORDERS[0], None, small_out, small_land, small_send, small_recv).advance(k)
+
+        for first, count, left, right, out, loads in groups:
+            @pl.when(t == first)
+            def _():
+                for load in loads:
+                    load.wait()
+
+            @pl.when((t >= first) & (t < first + count))
+            def _():
+                value = dot_tn(part(left, t - first), part(right, t - first))
+                buf[2 * t] = value[:256]
+                buf[2 * t + 1] = value[256:]
+
+        @pl.when(t == 0)
+        def _():
+            for g in range(gpos_ref.shape[0]):
+                for h in range(HEAD_GROUP):
+                    pos_s[:, g * HEAD_GROUP + h, :] = gpos_ref[g, :, h * seq:(h + 1) * seq]
+
+        @pl.when((t >= 1) & (t < 1 + table_ticks))
+        def _():
+            add_table(pos_s, idx_ref, table_s, (t - 1) * TABLE_STEP)
+
+        @pl.when(t == 1 + table_ticks)
+        def _():
+            summed = table_s[0:n_heads] + table_s[n_heads:2 * n_heads] + table_s[2 * n_heads:3 * n_heads]
+            for p in range(table_s.shape[1] // 128):
+                small_out[room + p * n_heads:room + (p + 1) * n_heads, :] = summed[:, p * 128:(p + 1) * 128]
+        return carry
+    lax.fori_loop(0, max(slots + STARTS[10] + 1, small_at + 11), tick, 0)
+
+    def drain(s, carry):
+        pltpu.make_async_copy(buf.at[s], block(outs[0], 0, 0), sem_out.at[s]).wait()
+        return carry
+    lax.fori_loop(0, total, drain, 0)
+
+
+def reduce_all(pairs, small, g_pos, idx_t, n_heads):
+    shapes = [(a.shape[1], b.shape[1]) for a, b in pairs]
+    total = sum(a * b // (256 * WIDTH) for a, b in shapes)
+    n = len(pairs)
+    flat = [x for pair in pairs for x in pair]
+    seq = idx_t.shape[0]
+    table_pad = (256 - small.shape[0]) * 128 // n_heads
+    vmem, hbm = pl.BlockSpec(memory_space=pltpu.VMEM), pl.BlockSpec(memory_space=pl.ANY)
+    outs = [sds(shape, F32) for shape in shapes] + [sds((256, 128), F32)]
+    dma = pltpu.SemaphoreType.DMA
+    return pl.pallas_call(
+        functools.partial(reduce_kernel, n=n), in_specs=[hbm] * (2 * n) + [vmem] * 3, out_specs=[hbm] * n + [vmem], out_shape=outs,
+        scratch_shapes=[pltpu.VMEM(x.shape, x.dtype) for x in flat] + [
+            pltpu.VMEM((total, 256, WIDTH), F32), pltpu.VMEM((total, 248, WIDTH), F32), pltpu.VMEM((248, 128), F32), pltpu.VMEM((seq, n_heads, seq), F32),
+            pltpu.VMEM((3 * n_heads, table_pad), F32), dma((total, 10)), dma((total, 10)), dma((10,)), dma((10,)), dma((2 * n,)), dma((total,))],
+        name="reduce", compiler_params=pltpu.CompilerParams(collective_id=0, has_side_effects=True, vmem_limit_bytes=63 * 1024 * 1024))(*flat, small, g_pos, idx_t)
+
+
+def unpack_small(small, shapes):
+    (s_nm, s_wr, s_na, s_wq, s_bq, s_table, s_wp, s_bp, s_nb, s_w1, s_b1, s_w2, s_b2) = shapes
+    flat = small.reshape(-1)
+    got, at = [], 0
+    for shape in (s_nm, s_na, s_nb, s_bq, s_bp, s_b1, s_b2):
+        size = math.prod(shape)
+        got.append(flat[at:at + size].reshape(shape))
+        at += size
+    pad = -(-s_table[0] // 128) * 128
+    rows = s_table[1] * pad // 128
+    g_table = small[256 - rows:].reshape(pad // 128, s_table[1], 128).transpose(0, 2, 1).reshape(pad, s_table[1])[:s_table[0]]
+    return got + [g_table]
 
 
 def solution(mesh):
     def device_fn(tokens, grad_out, rel_index, *weights):
         nb = mesh.shape['sp']
         cot = lax.all_to_all(grad_out, 'sp', 1, 0, tiled=True)
-        result, g_tok, grads = local_step(tokens, cot, rel_index, weights)
+        result, g_tok, grads, small, g_pos, idx_t = local_step(tokens, cot, rel_index, weights)
         result = lax.all_to_all(result.reshape(cot.shape), 'sp', 0, 1, tiled=True)
-        total = lax.psum(grads, ('dp', 'sp'))
-        return (result, g_tok) + tuple(total)
+        g_w2, g_w1, g_wr, g_wq, g_wp, small = reduce_all(grads, small, g_pos, idx_t, weights[5].shape[1])
+        g_nm, g_na, g_nb, g_bq, g_bp, g_b1, g_b2, g_table = unpack_small(small, [w.shape for w in weights])
+        return result, g_tok, g_nm, g_wr, g_na, g_wq, g_bq, g_table, g_wp, g_bp, g_nb, g_w1, g_b1, g_w2, g_b2
 
     rep_specs = (P(),) * 13
     return jax.shard_map(device_fn, mesh=mesh, in_specs=(P('dp', 'sp'), P(('dp', 'sp')), P()) + rep_specs, out_specs=(P(('dp', 'sp')), P('dp', 'sp')) + rep_specs, check_vma=False)

time: 553 us -> 261 us (0.47)
  waiting for transfers between devices: 374 us -> 0.01 us
  Pallas kernels: 112 us -> 219 us
  blocking collectives: 19.5 us -> 0 us
  between operations: 14.2 us -> 0.82 us
  local copies, waits for them, and re-layouts: 24.5 us -> 30.3 us
    psum x2 -> x0, waiting for transfers between devices: 374 us -> none  [device_fn(): total = lax.psum(grads, ('dp', 'sp'))]
    pallas_call x0 -> x1, Pallas kernels: none -> 140 us  [reduce_all(): pl.pallas_call(functools.partial(reduce_kernel, n=n), in_specs=[hbm] * (2...]
    pallas_call x5 -> x4, Pallas kernels: 112 us -> 78.7 us  [call(): pl.pallas_call(kernel, grid=grid, in_specs=in_specs, out_specs=out_specs,...]
    all_to_all x1 -> x0, blocking collectives: 19.5 us -> none  [device_fn(): result = lax.all_to_all(result.reshape(cot.shape), 'sp', 0, 1, tiled=True)]
    unnamed x59 -> x44, local copies, waits for them, and re-layouts: 17.7 us -> 20 us
  transfers between devices with their start and end apart: 3 -> 2, of which waited for: 2 -> 0; matrix products, arithmetic and copies ran while one was open for 1% -> 6% of each run, Pallas kernels for 5% -> 76%
where the time goes in v3:
time: 261 us; the launch traced here: 260 us
  Pallas kernels  219 us (84%)
  local copies, waits for them, and re-layouts  30.3 us (12%)
  starting transfers between devices  8.87 us (3%)
    pallas_call x1, Pallas kernels, reduce_all(): pl.pallas_call(functools.partial(reduce_kernel, n=n), in_specs=[hbm] * (2...  140 us
    pallas_call x4, Pallas kernels, call(): pl.pallas_call(kernel, grid=grid, in_specs=in_specs, out_specs=out_specs,...  78.7 us
    unnamed x44, local copies, waits for them, and re-layouts  20 us
  transfers between devices with their start and end apart: 2, of which 0 were waited for; matrix products, arithmetic and copies ran while one was open for 6% of the time, Pallas kernels for 76%

profile of v3, /device:TPU:0, one launch (start us, length us, event | category | flops | bytes accessed | tf_op | source)
XLA Modules:
  0.0 260.2 jit_solution(10850860267713419097)
XLA Ops:
  0.7 4.4 %all-to-all-start = ((bf16[1,48,24,512]{3,2,0,1:T(8,128)(2,1)}), bf16[1,48,24,512]{3,2,0,1:T(8,128)(2,1)S(1)}, u32[]{:S(2)}, u32[]{:S(2)}) async-start(bf16[1,48,24,512]{3,2,0,1:T(8,128)(2,1)} %bitcast.57), calls=%async_computation | async-start | bytes 2359296 | tf_op jit(solution)/shard_map/all_to_all | solution.py:540
  7.5 0.8 copy.37
  8.9 10.7 %pos.1.pos_ref = f32[2,144,1152]{2,1,0:T(8,128)} custom-call(f32[16,640]{1,0:T(8,128)} %pad_convert_fusion.table_ref, s32[144,144]{1,0:T(8,128)} %bitcast.49), custom_call_target="tpu_custom_call" | custom-call | flops 10000000 | bytes 1451008 | tf_op jit(solution)/shard_map/pos/pallas_call | solution.py:248
  19.6 19.4 %fwd.1 = (bf16[4,288,1024]{2,1,0:T(8,128)(2,1)}, bf16[4,288,512]{2,1,0:T(8,128)(2,1)}, bf16[4,288,1536]{2,1,0:T(8,128)(2,1)}, bf16[4,288,512]{2,1,0:T(8,128)(2,1...) custom-call(bf16[4,24,48,256]{3,2,1,0:T(8,128)(2,1)} %tok_ref.1, ...), custom_call_target="tpu_custom_call" | custom-call | flops 8000000000 | bytes 16648192 | tf_op jit(solution)/shard_map/fwd/pallas_call | solution.py:248
  39.0 1.0 copy-done.4
  40.0 20.3 %mlp.1 = (bf16[4,288,512]{2,1,0:T(8,128)(2,1)}, f32[4,288,512]{2,1,0:T(8,128)}, bf16[4,288,2048]{2,1,0:T(8,128)(2,1)}, bf16[4,288,2048]{2,1,0:T(8,128)(2,1)}, bf...) custom-call(bf16[4,288,512]{2,1,0:T(8,128)(2,1)} %get-tuple-element., ...), custom_call_target="tpu_custom_call" | custom-call | flops 12000000000 | bytes 22076416 | tf_op jit(solution)/shard_map/mlp/pallas_call | solution.py:248
  61.0 4.5 %all-to-all-start.1 = ((bf16[4,12,24,512]{3,2,1,0:T(8,128)(2,1)}), bf16[4,12,24,512]{3,2,1,0:T(8,128)(2,1)}, u32[]{:S(2)}, u32[]{:S(2)}) async-start(bf16[4,12,24,512]{3,2,1,0:T(8,128)(2,1)} %bitcast.58), calls=%async_computation.1 | async-start | bytes 2359296 | tf_op jit(solution)/shard_map/all_to_all | solution.py:542
  65.5 28.3 %bwd.1 = (bf16[4,24,48,256]{3,2,1,0:T(8,128)(2,1)}, bf16[4,288,512]{2,1,0:T(8,128)(2,1)}, bf16[4,288,512]{2,1,0:T(8,128)(2,1)}, bf16[4,288,1536]{2,1,0:T(8,128)(...) custom-call(f32[4,288,512]{2,1,0:T(8,128)} %get-tuple-element.49.dh1, ...), custom_call_target="tpu_custom_call" | custom-call | flops 12000000000 | bytes 27428864 | tf_op jit(solution)/shard_map/bwd/pallas_call | solution.py:248
  94.5 0.7 bitcast_dynamic-update-slice_fusion
  95.2 0.7 reduce.1
  97.3 140.1 %reduce.2 = (f32[2048,512]{1,0:T(8,128)}, f32[512,2048]{1,0:T(8,128)}, f32[1024,512]{1,0:T(8,128)}, f32[512,1536]{1,0:T(8,128)}, f32[512,512]{1,0:T(8,128)}, /*index=5*/f32[256,128]{1,0:T(8,128)}) custom-call(bf16[1152,2048]{1,0:T(8,128)(2,1)} %bitcast.45, bf16[1152,512]{1,0:T(8,128)(2,1)} %bitcast.53, bf16[1152,512]{1,0:T(8,128)(2,1)} %bitcast.52, ...), custom_call_target="tpu_custom_call" | custom-call | tf_op jit(solution)/shard_map/reduce/pallas_call | solution.py:515
  237.5 0.9 slice.46
  240.3 1.3 slice_bitcast_fusion
  242.8 1.3 slice_bitcast_fusion.2
  244.1 1.3 slice_bitcast_fusion.1
  245.4 2.4 copy.59
  247.8 1.3 copy.60
  249.1 1.3 copy-done.2
  250.4 1.7 copy.61
  252.4 1.0 copy.62
  253.3 1.1 copy-done.1
  254.4 2.1 copy.63
  256.6 1.6 copy-done
  258.1 2.0 copy.64
  (46 shorter events, 9.2 us)
Async XLA Ops:
  0.6 4.5 %copy-start.12 = (bf16[512]{0:T(512)(128)(2,1)S(1)}, bf16[512]{0:T(512)(128)(2,1)}, u32[]{:S(2)}) copy-start(bf16[512]{0:T(512)(128)(2,1)} %param.28) | copy-start | bytes 3076
  0.7 5.0 %copy-start.13 = (bf16[512]{0:T(512)(128)(2,1)S(1)}, bf16[512]{0:T(512)(128)(2,1)}, u32[]{:S(2)}) copy-start(bf16[512]{0:T(512)(128)(2,1)} %param.33) | copy-start | bytes 3076
  0.7 5.6 %copy-start.10 = (bf16[1536]{0:T(1024)(128)(2,1)S(1)}, bf16[1536]{0:T(1024)(128)(2,1)}, u32[]{:S(2)}) copy-start(bf16[1536]{0:T(1024)(128)(2,1)} %param.25) | copy-start | bytes 9220
  0.7 6.2 %copy-start.9 = (bf16[2048]{0:T(1024)(128)(2,1)S(1)}, bf16[2048]{0:T(1024)(128)(2,1)}, u32[]{:S(2)}) copy-start(bf16[2048]{0:T(1024)(128)(2,1)} %param.31) | copy-start | bytes 12292
  0.7 6.8 %copy-start.6 = (s32[144,144]{1,0:T(8,128)S(1)}, s32[144,144]{1,0:T(8,128)}, u32[]{:S(2)}) copy-start(s32[144,144]{1,0:T(8,128)} %param.20) | copy-start | bytes 248836
  0.7 7.6 %copy-start.7 = (bf16[529,16]{0,1:T(8,128)(2,1)S(1)}, bf16[529,16]{0,1:T(8,128)(2,1)}, u32[]{:S(2)}) copy-start(bf16[529,16]{0,1:T(8,128)(2,1)} %param.26) | copy-start | bytes 50788
  0.7 38.3 %all-to-all-start = ((bf16[1,48,24,512]{3,2,0,1:T(8,128)(2,1)}), bf16[1,48,24,512]{3,2,0,1:T(8,128)(2,1)S(1)}, u32[]{:S(2)}, u32[]{:S(2)}) async-start(bf16[1,48,24,512]{3,2,0,1:T(8,128)(2,1)} %bitcast.57), calls=%async_computation | async-start | bytes 2359296 | tf_op jit(solution)/shard_map/all_to_all | solution.py:540
  39.0 1.0 copy-start.4
  61.0 184.4 %all-to-all-start.1 = ((bf16[4,12,24,512]{3,2,1,0:T(8,128)(2,1)}), bf16[4,12,24,512]{3,2,1,0:T(8,128)(2,1)}, u32[]{:S(2)}, u32[]{:S(2)}) async-start(bf16[4,12,24,512]{3,2,1,0:T(8,128)(2,1)} %bitcast.58), calls=%async_computation.1 | async-start | bytes 2359296 | tf_op jit(solution)/shard_map/all_to_all | solution.py:542
  65.5 31.2 %copy-start.8 = (f32[1,2048]{1,0:T(1,128)S(1)}, f32[1,2048]{1,0:T(1,128)}, u32[]{:S(2)}) copy-start(f32[1,2048]{1,0:T(1,128)} %get-tuple-element.70) | copy-start | bytes 24580
  65.5 31.2 %copy-start.11 = (f32[1,512]{1,0:T(1,128)S(1)}, f32[1,512]{1,0:T(1,128)}, u32[]{:S(2)}) copy-start(f32[1,512]{1,0:T(1,128)} %get-tuple-element.71) | copy-start | bytes 6148
  237.4 10.3 %copy-start.3 = (f32[1024,512]{1,0:T(8,128)S(1)}, f32[1024,512]{1,0:T(8,128)}, u32[]{:S(2)}) copy-start(f32[1024,512]{1,0:T(8,128)} %get-tuple-element.103) | copy-start | bytes 6291460
  247.8 2.6 %copy-start.2 = (f32[512,1536]{1,0:T(8,128)S(1)}, f32[512,1536]{1,0:T(8,128)}, u32[]{:S(2)}) copy-start(f32[512,1536]{1,0:T(8,128)} %get-tuple-element.105) | copy-start | bytes 9437188
  250.4 2.0 copy-start.5
  250.4 4.0 %copy-start.1 = (f32[512,2048]{1,0:T(8,128)S(1)}, f32[512,2048]{1,0:T(8,128)}, u32[]{:S(2)}) copy-start(f32[512,2048]{1,0:T(8,128)} %get-tuple-element.111) | copy-start | bytes 12582916
  254.4 3.7 %copy-start = (f32[2048,512]{1,0:T(8,128)S(1)}, f32[2048,512]{1,0:T(8,128)}, u32[]{:S(2)}) copy-start(f32[2048,512]{1,0:T(8,128)} %get-tuple-element.113) | copy-start | bytes 12582916

commit v4 on v3

--- a/solution.py
+++ b/solution.py
@@ -67,7 +67,7 @@
     seq = idx_ref.shape[0]
     n_pieces = table_ref.shape[1] // 128
     for g in range(pos_ref.shape[0]):
-        wide = jnp.concatenate([idx_ref[...]] * HEAD_GROUP, axis=1)
+        wide = jnp.concatenate([idx_ref[...].T] * HEAD_GROUP, axis=1)
         for c in range(wide.shape[1] // 128):
             idx = wide[:, c * 128:(c + 1) * 128]
             low, high = idx & 127, idx >> 7
@@ -99,7 +99,7 @@
     h0 = dot_nn(merged, wr_ref[...]).astype(BF)
     h0_ref[0] = h0
     a = norm_fwd(h0.astype(F32), na_ref)[0].astype(BF)
-    qkv_ref[0] = (dot_nn(a, wq_ref[...]) + bq_ref[...].astype(F32)).astype(BF)
+    qkv_ref[0] = (dot_nn(a, wq_ref[...]) + bq_ref[...].astype(F32).reshape(1, -1)).astype(BF)
     width = HEAD_GROUP * head_dim
     masks, masks_f = head_masks(width, head_dim, BF), head_masks(width, head_dim, F32)
     scale = head_dim ** -0.5
@@ -115,7 +115,7 @@
             prob = (e * (1.0 / den)).astype(BF)
             lse_ref[0, w, g] = top + jnp.log(den)
             att_ref[0, rows, g * width:(g + 1) * width] = unstack_heads(dot_tn(prob, v), masks_f, seq).astype(BF)
-    h1 = h0_ref[0].astype(F32) + dot_nn(att_ref[0], wp_ref[...]) + bp_ref[...].astype(F32)
+    h1 = h0_ref[0].astype(F32) + dot_nn(att_ref[0], wp_ref[...]) + bp_ref[...].astype(F32).reshape(1, -1)
     h1_ref[0] = h1.astype(BF)
 
 
@@ -137,12 +137,12 @@
     cot_bf = cot.astype(BF)
     cotw_ref[0] = cot_bf
     gb2_ref[...] += jnp.sum(cot, axis=0, keepdims=True)
-    out = h1 + b2_ref[...].astype(F32)
+    out = h1 + b2_ref[...].astype(F32).reshape(1, -1)
     d_norm = jnp.zeros(h1.shape, F32)
     chunk = 512
     for c in range(w1_ref.shape[1] // chunk):
         cols = slice(c * chunk, (c + 1) * chunk)
-        pre = dot_nn(nb, w1_ref[:, cols]) + b1_ref[:, cols].astype(F32)
+        pre = dot_nn(nb, w1_ref[:, cols]) + b1_ref[cols].astype(F32).reshape(1, -1)
         phi = 0.5 + 0.5 * lax.erf(pre * math.sqrt(0.5))
         hid = (pre * phi).astype(BF)
         hid_ref[0, :, cols] = hid
@@ -290,20 +290,18 @@
     table_pad = -(-rel_table.shape[0] // 128) * 128
     perm4, perm_w = merge_perm(window, tok_cols), window_perm(window)
     table_t = jnp.pad(rel_table.astype(F32).T, ((0, 0), (0, table_pad - rel_table.shape[0])))
-    idx_t = rel_index.T
-    row = lambda x: x.reshape(1, -1)
-
-    pos = call(pos_kernel, (1,), (table_t, idx_t), [whole(table_t.shape), whole(idx_t.shape)],
+
+    pos = call(pos_kernel, (1,), (table_t, rel_index), [whole(table_t.shape), whole(rel_index.shape)],
                [sds((groups, seq, lanes), F32)], [out_whole((groups, seq, lanes))], [], 10**7, "pos")[0]
 
-    ins = (tokens, perm4, pos, norm_merge, w_reduce, norm_attn, w_qkv, row(b_qkv), w_proj, row(b_proj))
+    ins = (tokens, perm4, pos, norm_merge, w_reduce, norm_attn, w_qkv, b_qkv, w_proj, b_proj)
     outs = [sds((nb, n, 4 * chan), BF), sds((nb, n, dim), BF), sds((nb, n, 3 * dim), BF), sds((nb, n, dim), BF),
             sds((nb, 2, groups, 1, lanes), F32), sds((nb, n, dim), BF)]
     raw, h0, qkv, att, lse, h1 = call(
         functools.partial(fwd_kernel, head_dim=head_dim, seq=seq), (nb,), ins,
         [band(tokens.shape)] + [whole(a.shape) for a in ins[1:]], outs, [band(o.shape) for o in outs], [], 8 * 10**9, "fwd")
 
-    ins = (h1, cot.reshape(nb, n, dim), perm_w, norm_mlp, w_fc1, row(b_fc1), w_fc2, row(b_fc2))
+    ins = (h1, cot.reshape(nb, n, dim), perm_w, norm_mlp, w_fc1, b_fc1, w_fc2, b_fc2)
     tok = lambda width, dtype=BF: sds((nb, n, width), dtype)
     outs = [tok(dim), tok(dim, F32), tok(ff), tok(ff), tok(dim), tok(dim), sds((1, ff), F32), sds((1, dim), F32), sds((2, dim), F32)]
     result, dh1, hid, dpre, b_in, cot_w, g_b1, g_b2, g_nb = call(
@@ -319,11 +317,8 @@
         outs, [band(o.shape) for o in outs[:6]] + [out_whole(o.shape) for o in outs[6:]],
         [pltpu.VMEM((n, dim), BF), pltpu.VMEM((n, 3 * dim), F32)], 12 * 10**9, "bwd")
 
-    small = jnp.concatenate([x.reshape(-1) for x in (g_nm, g_na, g_nb, g_bq, g_bp, g_b1, g_b2)])
-    room = 256 - n_heads * table_pad // 128
-    small = jnp.pad(small, (0, room * 128 - small.shape[0])).reshape(room, 128)
     pairs = [(hid, cot_w), (b_in, dpre), (m_in, dh0), (a_in, dqkv), (att, dh1_bf)]
-    return result, g_tok, [tuple(x.reshape(nb * n, -1) for x in pair) for pair in pairs], small, g_pos, idx_t
+    return result, g_tok, [tuple(x.reshape(nb * n, -1) for x in pair) for pair in pairs], [g_nm, g_na, g_nb, g_bq, g_bp, g_b1, g_b2], g_pos
 
 
 ORDERS = (('core', 'x', 'y', 'z0', 'z1'), ('core', 'y', 'x', 'z0', 'z1'), ('core', 'z0', 'z1', 'x', 'y'), ('core', 'z0', 'z1', 'y', 'x'))
@@ -407,11 +402,12 @@
     table_s[...] = acc
 
 
-def reduce_kernel(*refs, n):
-    pairs, (small_in, gpos_ref, idx_ref) = refs[:2 * n], refs[2 * n:2 * n + 3]
-    outs, small_out = refs[2 * n + 3:3 * n + 3], refs[3 * n + 3]
-    held = refs[3 * n + 4:5 * n + 4]
-    buf, land, small_land, pos_s, table_s, send, recv, small_send, small_recv, sem_in, sem_out = refs[5 * n + 4:]
+def reduce_kernel(*refs, n, n_small):
+    refs = list(refs)
+    take = lambda count: [refs.pop(0) for _ in range(count)]
+    pairs, smalls, (gpos_ref, idx_ref, res_in) = take(2 * n), take(n_small), take(3)
+    outs, (small_out, res_out), held = take(n), take(2), take(2 * n)
+    buf, land, small_land, pos_s, table_s, idx_s, send, recv, small_send, small_recv, sem_in, sem_out, res_send, res_recv, res_here = refs
     seq = idx_ref.shape[0]
     n_heads = pos_s.shape[1]
     total = buf.shape[0]
@@ -433,13 +429,24 @@
         return ref[...] if ref.shape[1] == WIDTH else ref[:, pl.ds(pl.multiple_of(j * WIDTH, WIDTH), WIDTH)]
 
     peers = place()[1]
+    dp, sp = lax.axis_index('dp'), lax.axis_index('sp')
+    ring = res_in.shape[0]
     barrier = pltpu.get_barrier_semaphore()
-    for k in ORDERS[0]:
-        pl.semaphore_signal(barrier, inc=1, device_id=peers[k], device_id_type=pl.DeviceIdType.MESH)
-    pl.semaphore_wait(barrier, 5)
+    for peer in [peers[k] for k in ORDERS[0]] + [(dp, 3 - sp)]:
+        pl.semaphore_signal(barrier, inc=1, device_id=peer, device_id_type=pl.DeviceIdType.MESH)
+    pl.semaphore_wait(barrier, 6)
+    moves = [pltpu.make_async_copy(res_in.at[sp], res_out.at[sp], res_here.at[0])]
+    for d in range(1, ring):
+        to = lax.rem(sp + d, ring)
+        moves.append(pltpu.make_async_remote_copy(src_ref=res_in.at[to], dst_ref=res_out.at[sp], send_sem=res_send.at[d], recv_sem=res_recv.at[d],
+                                                  device_id=(dp, to), device_id_type=pl.DeviceIdType.MESH))
+    for move in moves:
+        move.start()
     table_s[...] = jnp.zeros(table_s.shape, F32)
-    room = small_in.shape[0]
-    small_out[0:room, :] = small_in[...]
+    room = small_out.shape[0] - table_s.shape[0] * table_s.shape[1] // (3 * 128)
+    small_out[0:room, :] = jnp.zeros((room, 128), F32)
+    for ref, r, c, at in small_rows([x.shape for x in smalls]):
+        small_out[at:at + 1, :] = smalls[ref][r:r + 1, c:c + 128]
     table_ticks = seq // TABLE_STEP
     small_at = table_ticks + 2
     slots = total // 2
@@ -480,13 +487,14 @@
 
         @pl.when(t == 0)
         def _():
+            idx_s[...] = idx_ref[...].T
             for g in range(gpos_ref.shape[0]):
                 for h in range(HEAD_GROUP):
                     pos_s[:, g * HEAD_GROUP + h, :] = gpos_ref[g, :, h * seq:(h + 1) * seq]
 
         @pl.when((t >= 1) & (t < 1 + table_ticks))
         def _():
-            add_table(pos_s, idx_ref, table_s, (t - 1) * TABLE_STEP)
+            add_table(pos_s, idx_s, table_s, (t - 1) * TABLE_STEP)
 
         @pl.when(t == 1 + table_ticks)
         def _():
@@ -500,49 +508,91 @@
         pltpu.make_async_copy(buf.at[s], block(outs[0], 0, 0), sem_out.at[s]).wait()
         return carry
     lax.fori_loop(0, total, drain, 0)
-
-
-def reduce_all(pairs, small, g_pos, idx_t, n_heads):
+    for move in moves:
+        move.wait()
+
+
+def small_rows(shapes):
+    rows = []
+    for ref, shape in enumerate(shapes):
+        for r in range(shape[0]):
+            for c in range(0, shape[1], 128):
+                rows.append((ref, r, c, len(rows)))
+    return rows
+
+
+def reduce_all(pairs, smalls, g_pos, rel_index, result, n_heads, table_len):
     shapes = [(a.shape[1], b.shape[1]) for a, b in pairs]
     total = sum(a * b // (256 * WIDTH) for a, b in shapes)
     n = len(pairs)
     flat = [x for pair in pairs for x in pair]
-    seq = idx_t.shape[0]
-    table_pad = (256 - small.shape[0]) * 128 // n_heads
+    seq = rel_index.shape[0]
+    table_pad = -(-table_len // 128) * 128
     vmem, hbm = pl.BlockSpec(memory_space=pltpu.VMEM), pl.BlockSpec(memory_space=pl.ANY)
-    outs = [sds(shape, F32) for shape in shapes] + [sds((256, 128), F32)]
+    outs = [sds(shape, F32) for shape in shapes] + [sds((256, 128), F32), sds(result.shape, result.dtype)]
     dma = pltpu.SemaphoreType.DMA
+    ring = result.shape[0]
     return pl.pallas_call(
-        functools.partial(reduce_kernel, n=n), in_specs=[hbm] * (2 * n) + [vmem] * 3, out_specs=[hbm] * n + [vmem], out_shape=outs,
+        functools.partial(reduce_kernel, n=n, n_small=len(smalls)),
+        in_specs=[hbm] * (2 * n) + [vmem] * (len(smalls) + 2) + [hbm], out_specs=[hbm] * n + [vmem, hbm], out_shape=outs,
         scratch_shapes=[pltpu.VMEM(x.shape, x.dtype) for x in flat] + [
             pltpu.VMEM((total, 256, WIDTH), F32), pltpu.VMEM((total, 248, WIDTH), F32), pltpu.VMEM((248, 128), F32), pltpu.VMEM((seq, n_heads, seq), F32),
-            pltpu.VMEM((3 * n_heads, table_pad), F32), dma((total, 10)), dma((total, 10)), dma((10,)), dma((10,)), dma((2 * n,)), dma((total,))],
-        name="reduce", compiler_params=pltpu.CompilerParams(collective_id=0, has_side_effects=True, vmem_limit_bytes=63 * 1024 * 1024))(*flat, small, g_pos, idx_t)
-
-
-def unpack_small(small, shapes):
-    (s_nm, s_wr, s_na, s_wq, s_bq, s_table, s_wp, s_bp, s_nb, s_w1, s_b1, s_w2, s_b2) = shapes
-    flat = small.reshape(-1)
-    got, at = [], 0
-    for shape in (s_nm, s_na, s_nb, s_bq, s_bp, s_b1, s_b2):
-        size = math.prod(shape)
-        got.append(flat[at:at + size].reshape(shape))
-        at += size
-    pad = -(-s_table[0] // 128) * 128
-    rows = s_table[1] * pad // 128
-    g_table = small[256 - rows:].reshape(pad // 128, s_table[1], 128).transpose(0, 2, 1).reshape(pad, s_table[1])[:s_table[0]]
-    return got + [g_table]
+            pltpu.VMEM((3 * n_heads, table_pad), F32), pltpu.VMEM((seq, seq), jnp.int32), dma((total, 10)), dma((total, 10)), dma((10,)), dma((10,)),
+            dma((2 * n,)), dma((total,)), dma((ring,)), dma((ring,)), dma((1,))],
+        name="reduce", compiler_params=pltpu.CompilerParams(collective_id=0, has_side_effects=True, vmem_limit_bytes=63 * 1024 * 1024))(
+            *flat, *smalls, g_pos, rel_index, result)
+
+
+def finish_kernel(*refs, n, cuts):
+    refs = list(refs)
+    take = lambda count: [refs.pop(0) for _ in range(count)]
+    ins, (small,), outs, smalls, (table,), bufs, (sem_in, sem_out) = take(n), take(1), take(n), take(len(refs) - n - 3), take(1), take(n), refs
+    stores = []
+    loads = []
+    for i, (a, b, c) in enumerate(zip(ins, bufs, outs)):
+        step = a.shape[0] // cuts
+        for p in range(cuts):
+            at = pl.ds(p * step, step)
+            loads.append(pltpu.make_async_copy(a.at[at], b.at[at], sem_in.at[i, p]))
+            stores.append(pltpu.make_async_copy(b.at[at], c.at[at], sem_out.at[i, p]))
+    for load in loads:
+        load.start()
+    for ref, r, c, at in small_rows([x.shape for x in smalls]):
+        smalls[ref][r:r + 1, c:c + 128] = small[at:at + 1, :]
+    n_heads, table_len = table.shape
+    pieces = -(-table_len // 128)
+    first = small.shape[0] - pieces * n_heads
+    full = jnp.concatenate([small[first + p * n_heads:first + (p + 1) * n_heads, :] for p in range(pieces)], axis=1)
+    table[...] = full[:, :table_len]
+    for load, store in zip(loads, stores):
+        load.wait()
+        store.start()
+    for store in stores:
+        store.wait()
+
+
+def finish(large, small, small_shapes, n_heads, table_len):
+    n, cuts = len(large), 4
+    vmem, hbm = pl.BlockSpec(memory_space=pltpu.VMEM), pl.BlockSpec(memory_space=pl.ANY)
+    outs = [sds(x.shape, x.dtype) for x in large] + [sds(shape, F32) for shape in small_shapes] + [sds((n_heads, table_len), F32)]
+    got = pl.pallas_call(
+        functools.partial(finish_kernel, n=n, cuts=cuts), in_specs=[hbm] * n + [vmem], out_specs=[hbm] * n + [vmem] * (len(outs) - n), out_shape=outs,
+        scratch_shapes=[pltpu.VMEM(x.shape, x.dtype) for x in large] + [pltpu.SemaphoreType.DMA((n, cuts)), pltpu.SemaphoreType.DMA((n, cuts))],
+        name="finish", compiler_params=pltpu.CompilerParams(vmem_limit_bytes=VMEM_LIMIT))(*large, small)
+    return got[:n], got[n:-1], got[-1].T
 
 
 def solution(mesh):
     def device_fn(tokens, grad_out, rel_index, *weights):
-        nb = mesh.shape['sp']
         cot = lax.all_to_all(grad_out, 'sp', 1, 0, tiled=True)
-        result, g_tok, grads, small, g_pos, idx_t = local_step(tokens, cot, rel_index, weights)
-        result = lax.all_to_all(result.reshape(cot.shape), 'sp', 0, 1, tiled=True)
-        g_w2, g_w1, g_wr, g_wq, g_wp, small = reduce_all(grads, small, g_pos, idx_t, weights[5].shape[1])
-        g_nm, g_na, g_nb, g_bq, g_bp, g_b1, g_b2, g_table = unpack_small(small, [w.shape for w in weights])
-        return result, g_tok, g_nm, g_wr, g_na, g_wq, g_bq, g_table, g_wp, g_bp, g_nb, g_w1, g_b1, g_w2, g_b2
+        result, g_tok, pairs, smalls, g_pos = local_step(tokens, cot, rel_index, weights)
+        table_len, n_heads = weights[5].shape
+        *grads, small, result = reduce_all(pairs, smalls, g_pos, rel_index, result, n_heads, table_len)
+        large, smalls, g_table = finish(grads + [result], small, [x.shape for x in smalls], n_heads, table_len)
+        g_w2, g_w1, g_wr, g_wq, g_wp, result = large
+        g_nm, g_na, g_nb, g_bq, g_bp, g_b1, g_b2 = smalls
+        return (result.reshape(grad_out.shape), g_tok, g_nm, g_wr, g_na, g_wq, g_bq.reshape(-1), g_table, g_wp, g_bp.reshape(-1), g_nb,
+                g_w1, g_b1.reshape(-1), g_w2, g_b2.reshape(-1))
 
     rep_specs = (P(),) * 13
     return jax.shard_map(device_fn, mesh=mesh, in_specs=(P('dp', 'sp'), P(('dp', 'sp')), P()) + rep_specs, out_specs=(P(('dp', 'sp')), P('dp', 'sp')) + rep_specs, check_vma=False)

time: 261 us -> 245 us (0.939)
  local copies, waits for them, and re-layouts: 30.3 us -> 1.01 us
  Pallas kernels: 219 us -> 236 us
  starting transfers between devices: 8.87 us -> 4.28 us
    unnamed x44 -> x4, local copies, waits for them, and re-layouts: 20 us -> 1.01 us
    pallas_call x1 -> x2, Pallas kernels: 140 us -> 157 us  [the longest x1 144 us: reduce_all(): pl.pallas_call(functools.partial(reduce_kernel, n=n, n_small=len(smalls))...]
    slice x5 -> x0, local copies, waits for them, and re-layouts: 5.49 us -> none  [the longest x4 4.55 us: unpack_small(): got.append(flat[at:at + size].reshape(shape))]
    reshape x9 -> x0, local copies, waits for them, and re-layouts: 4.84 us -> none  [the longest x4 2.36 us: local_step(): row = lambda x: x.reshape(1, -1)]
    all_to_all x1 -> x0, starting transfers between devices: 4.45 us -> none  [device_fn(): result = lax.all_to_all(result.reshape(cot.shape), 'sp', 0, 1, tiled=True)]
  transfers between devices with their start and end apart: 2 -> 1, of which waited for: 0 -> 0; matrix products, arithmetic and copies ran while one was open for 6% -> 0% of each run, Pallas kernels for 76% -> 12%
where the time goes in v4:
time: 245 us; the launch traced here: 244 us
  Pallas kernels  236 us (96%)
  starting transfers between devices  4.28 us (2%)
    pallas_call x1, Pallas kernels, reduce_all(): pl.pallas_call(functools.partial(reduce_kernel, n=n, n_small=len(smalls))...  144 us
    pallas_call x4, Pallas kernels, call(): pl.pallas_call(kernel, grid=grid, in_specs=in_specs, out_specs=out_specs,...  79.1 us
    pallas_call x1, Pallas kernels, finish(): pl.pallas_call(functools.partial(finish_kernel, n=n, cuts=cuts), in_specs...  13.2 us
  transfers between devices with their start and end apart: 1, of which 0 were waited for; matrix products, arithmetic and copies ran while one was open for 0% of the time, Pallas kernels for 12%

profile of v4, /device:TPU:0, one launch (start us, length us, event | category | flops | bytes accessed | tf_op | source)
XLA Modules:
  0.0 244.2 jit_solution(16656193772413487996)
XLA Ops:
  0.6 0.0 copy-start.1
  0.7 4.3 %all-to-all-start = ((bf16[1,48,24,512]{3,2,0,1:T(8,128)(2,1)}), bf16[1,48,24,512]{3,2,0,1:T(8,128)(2,1)S(1)}, u32[]{:S(2)}, u32[]{:S(2)}) async-start(bf16[1,48,24,512]{3,2,0,1:T(8,128)(2,1)} %bitcast.28), calls=%async_computation | async-start | bytes 2359296 | tf_op jit(solution)/shard_map/all_to_all | solution.py:587
  4.9 0.0 copy-done.1
  4.9 0.6 pad_convert_fusion.table_ref
  5.6 10.8 %pos.1.pos_ref = f32[2,144,1152]{2,1,0:T(8,128)} custom-call(f32[16,640]{1,0:T(8,128)} %pad_convert_fusion.table_ref, s32[144,144]{1,0:T(8,128)} %refs_18_.1), custom_call_target="tpu_custom_call" | custom-call | flops 10000000 | bytes 1451008 | tf_op jit(solution)/shard_map/pos/pallas_call | solution.py:248
  16.4 19.4 %fwd.1 = (bf16[4,288,1024]{2,1,0:T(8,128)(2,1)}, bf16[4,288,512]{2,1,0:T(8,128)(2,1)}, bf16[4,288,1536]{2,1,0:T(8,128)(2,1)}, bf16[4,288,512]{2,1,0:T(8,128)(2,1...) custom-call(bf16[4,24,48,256]{3,2,1,0:T(8,128)(2,1)} %tok_ref.1, ...), custom_call_target="tpu_custom_call" | custom-call | flops 8000000000 | bytes 16648192 | tf_op jit(solution)/shard_map/fwd/pallas_call | solution.py:248
  35.8 0.0 all-to-all-done
  35.8 0.0 copy-start
  35.8 1.0 copy-done
  36.8 20.5 %mlp.1 = (bf16[4,288,512]{2,1,0:T(8,128)(2,1)}, f32[4,288,512]{2,1,0:T(8,128)}, bf16[4,288,2048]{2,1,0:T(8,128)(2,1)}, bf16[4,288,2048]{2,1,0:T(8,128)(2,1)}, bf...) custom-call(bf16[4,288,512]{2,1,0:T(8,128)(2,1)} %get-tuple-element., ...), custom_call_target="tpu_custom_call" | custom-call | flops 12000000000 | bytes 22076416 | tf_op jit(solution)/shard_map/mlp/pallas_call | solution.py:248
  57.3 28.3 %bwd.1 = (bf16[4,24,48,256]{3,2,1,0:T(8,128)(2,1)}, bf16[4,288,512]{2,1,0:T(8,128)(2,1)}, bf16[4,288,512]{2,1,0:T(8,128)(2,1)}, bf16[4,288,1536]{2,1,0:T(8,128)(...) custom-call(f32[4,288,512]{2,1,0:T(8,128)} %get-tuple-element.67.dh1, ...), custom_call_target="tpu_custom_call" | custom-call | flops 12000000000 | bytes 27428864 | tf_op jit(solution)/shard_map/bwd/pallas_call | solution.py:248
  85.7 144.0 %reduce.2 = (f32[2048,512]{1,0:T(8,128)}, f32[512,2048]{1,0:T(8,128)}, f32[1024,512]{1,0:T(8,128)}, f32[512,1536]{1,0:T(8,128)}, f32[512,512]{1,0:T(8,128)}, /*i...) custom-call(bf16[1152,2048]{1,0:T(8,128)(2,1)} %bitcast.18, bf16[1152,512]{1,0:T(8,128)(2,1)} %bitcast.24, ...), custom_call_target="tpu_custom_call" | custom-call | tf_op jit(solution)/shard_map/reduce/pallas_call | solution.py:535
  229.7 13.2 %finish.1 = (f32[2048,512]{1,0:T(8,128)}, f32[512,2048]{1,0:T(8,128)}, f32[1024,512]{1,0:T(8,128)}, f32[512,1536]{1,0:T(8,128)}, f32[512,512]{1,0:T(8,128)}, /*i...) custom-call(f32[2048,512]{1,0:T(8,128)} %get-tuple-element.87.refs_0, ...), custom_call_target="tpu_custom_call" | custom-call | tf_op jit(solution)/shard_map/finish/pallas_call | solution.py:578
  242.9 1.3 reduce.1
Async XLA Ops:
  0.6 4.3 %copy-start.1 = (bf16[529,16]{0,1:T(8,128)(2,1)S(1)}, bf16[529,16]{0,1:T(8,128)(2,1)}, u32[]{:S(2)}) copy-start(bf16[529,16]{0,1:T(8,128)(2,1)} %param.26) | copy-start | bytes 50788
  0.7 35.2 %all-to-all-start = ((bf16[1,48,24,512]{3,2,0,1:T(8,128)(2,1)}), bf16[1,48,24,512]{3,2,0,1:T(8,128)(2,1)S(1)}, u32[]{:S(2)}, u32[]{:S(2)}) async-start(bf16[1,48,24,512]{3,2,0,1:T(8,128)(2,1)} %bitcast.28), calls=%async_computation | async-start | bytes 2359296 | tf_op jit(solution)/shard_map/all_to_all | solution.py:587
  35.8 1.0 copy-start

commit v5 on v4

--- a/solution.py
+++ b/solution.py
@@ -160,15 +160,15 @@
     dh1_ref[0] = cot + dx
 
 
-def bwd_kernel(dh1_ref, raw_ref, h0_ref, qkv_ref, lse_ref, perm_ref, pos_ref, nm_ref, wr_ref, na_ref, wq_ref, wp_ref,
-               gtok_ref, dh1b_ref, a_ref, dqkv_ref, m_ref, dh0_ref, gbp_ref, gbq_ref, gna_ref, gnm_ref, gpos_ref,
+def bwd_kernel(dh1_ref, h0_ref, qkv_ref, lse_ref, pos_ref, na_ref, wq_ref, wp_ref,
+               dh1b_ref, a_ref, dqkv_ref, dh0_ref, gbp_ref, gbq_ref, gna_ref, gpos_ref,
                datt_s, dqkv_f, *, head_dim, seq):
     i = pl.program_id(0)
     dim = h0_ref.shape[2]
 
     @pl.when(i == 0)
     def _():
-        for ref in (gbp_ref, gbq_ref, gna_ref, gnm_ref, gpos_ref):
+        for ref in (gbp_ref, gbq_ref, gna_ref, gpos_ref):
             ref[...] = jnp.zeros(ref.shape, F32)
 
     dh1 = dh1_ref[0]
@@ -206,22 +206,25 @@
     gna_ref[1:2, :] += g_shift
     dh0_bf = (dh1 + dx).astype(BF)
     dh0_ref[0] = dh0_bf
-    d_m = dot_nt(dh0_bf, wr_ref[...])
-    normed, hat, rstd = norm_fwd(raw_ref[0].astype(F32), nm_ref)
-    m_ref[0] = normed.astype(BF)
+
+
+def merge_backward(rows, raw_ref, dh0_ref, perm_ref, nm_ref, wr_ref, gnm_s, stage):
+    d_m = dot_nt(dh0_ref[rows, :], wr_ref[...])
+    normed, hat, rstd = norm_fwd(raw_ref[rows, :].astype(F32), nm_ref)
+    raw_ref[rows, :] = normed.astype(BF)
     dx, g_gain, g_shift = norm_bwd(d_m, hat, rstd, nm_ref)
-    gnm_ref[0:1, :] += g_gain
-    gnm_ref[1:2, :] += g_shift
+    gnm_s[0:1, :] += g_gain
+    gnm_s[1:2, :] += g_shift
     d_raw = dx.astype(BF)
     step = perm_ref.shape[0]
-    quad = step // 4
-    piece = quad // 2
+    piece = step // 8
+    seq = d_raw.shape[0] // 2
     chan = d_raw.shape[1] // 4
-    tok_rows = step // gtok_ref.shape[2]
+    tok_rows = step // stage.shape[1]
     for g in range(seq // piece):
         y = jnp.concatenate([d_raw[w * seq + g * piece:w * seq + (g + 1) * piece, p * chan:(p + 1) * chan]
                              for p in range(4) for w in range(2)], axis=0)
-        gtok_ref[0, g * tok_rows:(g + 1) * tok_rows] = dot_tn(perm_ref[...], y).astype(BF).reshape(tok_rows, gtok_ref.shape[2], chan)
+        stage[g * tok_rows:(g + 1) * tok_rows] = dot_tn(perm_ref[...], y).astype(BF).reshape(tok_rows, stage.shape[1], chan)
 
 
 def whole(shape):
@@ -308,17 +311,17 @@
         mlp_kernel, (nb,), ins, [band(ins[0].shape), band(ins[1].shape)] + [whole(a.shape) for a in ins[2:]],
         outs, [band(o.shape) for o in outs[:6]] + [out_whole(o.shape) for o in outs[6:]], [], 12 * 10**9, "mlp")
 
-    ins = (dh1, raw, h0, qkv, lse, perm4, pos, norm_merge, w_reduce, norm_attn, w_qkv, w_proj)
-    outs = [sds(tokens.shape, BF), tok(dim), tok(dim), tok(3 * dim), tok(4 * chan), tok(dim), sds((1, dim), F32),
-            sds((1, 3 * dim), F32), sds((2, dim), F32), sds((2, 4 * chan), F32), sds((groups, seq, lanes), F32)]
-    g_tok, dh1_bf, a_in, dqkv, m_in, dh0, g_bp, g_bq, g_na, g_nm, g_pos = call(
+    ins = (dh1, h0, qkv, lse, pos, norm_attn, w_qkv, w_proj)
+    outs = [tok(dim), tok(dim), tok(3 * dim), tok(dim), sds((1, dim), F32), sds((1, 3 * dim), F32), sds((2, dim), F32), sds((groups, seq, lanes), F32)]
+    dh1_bf, a_in, dqkv, dh0, g_bp, g_bq, g_na, g_pos = call(
         functools.partial(bwd_kernel, head_dim=head_dim, seq=seq), (nb,), ins,
-        [band(a.shape) for a in ins[:5]] + [whole(a.shape) for a in ins[5:]],
-        outs, [band(o.shape) for o in outs[:6]] + [out_whole(o.shape) for o in outs[6:]],
+        [band(a.shape) for a in ins[:4]] + [whole(a.shape) for a in ins[4:]],
+        outs, [band(o.shape) for o in outs[:4]] + [out_whole(o.shape) for o in outs[4:]],
         [pltpu.VMEM((n, dim), BF), pltpu.VMEM((n, 3 * dim), F32)], 12 * 10**9, "bwd")
 
-    pairs = [(hid, cot_w), (b_in, dpre), (m_in, dh0), (a_in, dqkv), (att, dh1_bf)]
-    return result, g_tok, [tuple(x.reshape(nb * n, -1) for x in pair) for pair in pairs], [g_nm, g_na, g_nb, g_bq, g_bp, g_b1, g_b2], g_pos
+    pairs = [(hid, cot_w), (b_in, dpre), (a_in, dqkv), (att, dh1_bf), (raw, dh0)]
+    return (result, [tuple(x.reshape(nb * n, -1) for x in pair) for pair in pairs], [g_na, g_nb, g_bq, g_bp, g_b1, g_b2],
+            [perm4, norm_merge, w_reduce, g_pos, rel_index])
 
 
 ORDERS = (('core', 'x', 'y', 'z0', 'z1'), ('core', 'y', 'x', 'z0', 'z1'), ('core', 'z0', 'z1', 'x', 'y'), ('core', 'z0', 'z1', 'y', 'x'))
@@ -327,7 +330,8 @@
 WIDTH = 512
 STARTS = tuple(range(1, 23, 2))
 Z_FIRST = 5
-TABLE_STEP = 8
+TABLE_STEP = 12
+TABLE_FROM = 9
 
 
 def place():
@@ -402,12 +406,12 @@
     table_s[...] = acc
 
 
-def reduce_kernel(*refs, n, n_small):
+def reduce_kernel(*refs, n, n_small, bands):
     refs = list(refs)
     take = lambda count: [refs.pop(0) for _ in range(count)]
-    pairs, smalls, (gpos_ref, idx_ref, res_in) = take(2 * n), take(n_small), take(3)
-    outs, (small_out, res_out), held = take(n), take(2), take(2 * n)
-    buf, land, small_land, pos_s, table_s, idx_s, send, recv, small_send, small_recv, sem_in, sem_out, res_send, res_recv, res_here = refs
+    pairs, smalls, (perm_ref, nm_ref, wr_ref, gpos_ref, idx_ref, res_in) = take(2 * n), take(n_small), take(6)
+    outs, (small_out, res_out, gtok_out), held = take(n), take(3), take(2 * n)
+    buf, land, small_land, pos_s, table_s, idx_s, send, recv, small_send, small_recv, sem_in, sem_out, res_send, res_recv, res_here, gnm_s, stage, sem_stage = refs
     seq = idx_ref.shape[0]
     n_heads = pos_s.shape[1]
     total = buf.shape[0]
@@ -445,10 +449,13 @@
     table_s[...] = jnp.zeros(table_s.shape, F32)
     room = small_out.shape[0] - table_s.shape[0] * table_s.shape[1] // (3 * 128)
     small_out[0:room, :] = jnp.zeros((room, 128), F32)
-    for ref, r, c, at in small_rows([x.shape for x in smalls]):
-        small_out[at:at + 1, :] = smalls[ref][r:r + 1, c:c + 128]
+    gnm_s[...] = jnp.zeros(gnm_s.shape, F32)
+    rows_of = small_rows([x.shape for x in smalls] + [gnm_s.shape])
+    for ref, r, c, at in rows_of:
+        if ref < n_small:
+            small_out[at:at + 1, :] = smalls[ref][r:r + 1, c:c + 128]
     table_ticks = seq // TABLE_STEP
-    small_at = table_ticks + 2
+    small_at = TABLE_FROM + table_ticks + 1
     slots = total // 2
 
     def tick(t, carry):
@@ -457,10 +464,9 @@
 
             @pl.when((u >= 0) & (u < slots))
             def _():
-                swap = lax.rem(u, Z_FIRST) == Z_FIRST - 1
                 for side in range(2):
                     s = 2 * u + side
-                    Stream(ORDERS[side], ORDERS[2 + side], swap, buf.at[s], land.at[s], send.at[s], recv.at[s]).advance(k)
+                    Stream(ORDERS[side], ORDERS[2 + side], lax.rem(u, Z_FIRST) == Z_FIRST - 1, buf.at[s], land.at[s], send.at[s], recv.at[s]).advance(k)
                 if k == 10:
                     for first, count, left, right, out, loads in groups:
                         @pl.when((u >= first) & (u < first + count))
@@ -474,7 +480,7 @@
                 Stream(ORDERS[0], ORDERS[0], None, small_out, small_land, small_send, small_recv).advance(k)
 
         for first, count, left, right, out, loads in groups:
-            @pl.when(t == first)
+            @pl.when(t == (first if left is not held[-2] else 1))
             def _():
                 for load in loads:
                     load.wait()
@@ -492,12 +498,27 @@
                 for h in range(HEAD_GROUP):
                     pos_s[:, g * HEAD_GROUP + h, :] = gpos_ref[g, :, h * seq:(h + 1) * seq]
 
-        @pl.when((t >= 1) & (t < 1 + table_ticks))
+        @pl.when((lax.rem(t, 2) == 1) & (t < 2 * bands))
         def _():
-            add_table(pos_s, idx_s, table_s, (t - 1) * TABLE_STEP)
-
-        @pl.when(t == 1 + table_ticks)
+            b = t // 2
+            size = held[-1].shape[0] // bands
+            store = pltpu.make_async_copy(stage, gtok_out.at[b], sem_stage.at[0])
+
+            @pl.when(b > 0)
+            def _():
+                store.wait()
+            merge_backward(pl.ds(pl.multiple_of(b * size, size), size), held[-2], held[-1], perm_ref, nm_ref, wr_ref, gnm_s, stage)
+            store.start()
+
+        @pl.when((t >= TABLE_FROM) & (t < TABLE_FROM + table_ticks))
         def _():
+            add_table(pos_s, idx_s, table_s, (t - TABLE_FROM) * TABLE_STEP)
+
+        @pl.when(t == TABLE_FROM + table_ticks)
+        def _():
+            for ref, r, c, at in rows_of:
+                if ref == n_small:
+                    small_out[at:at + 1, :] = gnm_s[r:r + 1, c:c + 128]
             summed = table_s[0:n_heads] + table_s[n_heads:2 * n_heads] + table_s[2 * n_heads:3 * n_heads]
             for p in range(table_s.shape[1] // 128):
                 small_out[room + p * n_heads:room + (p + 1) * n_heads, :] = summed[:, p * 128:(p + 1) * 128]
@@ -510,6 +531,7 @@
     lax.fori_loop(0, total, drain, 0)
     for move in moves:
         move.wait()
+    pltpu.make_async_copy(stage, gtok_out.at[bands - 1], sem_stage.at[0]).wait()
 
 
 def small_rows(shapes):
@@ -521,26 +543,27 @@
     return rows
 
 
-def reduce_all(pairs, smalls, g_pos, rel_index, result, n_heads, table_len):
+def reduce_all(pairs, smalls, extras, result, tokens, n_heads, table_len):
     shapes = [(a.shape[1], b.shape[1]) for a, b in pairs]
     total = sum(a * b // (256 * WIDTH) for a, b in shapes)
     n = len(pairs)
     flat = [x for pair in pairs for x in pair]
-    seq = rel_index.shape[0]
+    seq = extras[-1].shape[0]
     table_pad = -(-table_len // 128) * 128
     vmem, hbm = pl.BlockSpec(memory_space=pltpu.VMEM), pl.BlockSpec(memory_space=pl.ANY)
-    outs = [sds(shape, F32) for shape in shapes] + [sds((256, 128), F32), sds(result.shape, result.dtype)]
+    outs = [sds(shape, F32) for shape in shapes] + [sds((256, 128), F32), sds(result.shape, result.dtype), sds(tokens.shape, BF)]
     dma = pltpu.SemaphoreType.DMA
     ring = result.shape[0]
     return pl.pallas_call(
-        functools.partial(reduce_kernel, n=n, n_small=len(smalls)),
-        in_specs=[hbm] * (2 * n) + [vmem] * (len(smalls) + 2) + [hbm], out_specs=[hbm] * n + [vmem, hbm], out_shape=outs,
+        functools.partial(reduce_kernel, n=n, n_small=len(smalls), bands=tokens.shape[0]),
+        in_specs=[hbm] * (2 * n) + [vmem] * (len(smalls) + 5) + [hbm], out_specs=[hbm] * n + [vmem, hbm, hbm], out_shape=outs,
         scratch_shapes=[pltpu.VMEM(x.shape, x.dtype) for x in flat] + [
             pltpu.VMEM((total, 256, WIDTH), F32), pltpu.VMEM((total, 248, WIDTH), F32), pltpu.VMEM((248, 128), F32), pltpu.VMEM((seq, n_heads, seq), F32),
             pltpu.VMEM((3 * n_heads, table_pad), F32), pltpu.VMEM((seq, seq), jnp.int32), dma((total, 10)), dma((total, 10)), dma((10,)), dma((10,)),
-            dma((2 * n,)), dma((total,)), dma((ring,)), dma((ring,)), dma((1,))],
+            dma((2 * n,)), dma((total,)), dma((ring,)), dma((ring,)), dma((1,)),
+            pltpu.VMEM(extras[1].shape, F32), pltpu.VMEM(tokens.shape[1:], BF), dma((1,))],
         name="reduce", compiler_params=pltpu.CompilerParams(collective_id=0, has_side_effects=True, vmem_limit_bytes=63 * 1024 * 1024))(
-            *flat, *smalls, g_pos, rel_index, result)
+            *flat, *smalls, *extras, result)
 
 
 def finish_kernel(*refs, n, cuts):
@@ -585,12 +608,13 @@
 def solution(mesh):
     def device_fn(tokens, grad_out, rel_index, *weights):
         cot = lax.all_to_all(grad_out, 'sp', 1, 0, tiled=True)
-        result, g_tok, pairs, smalls, g_pos = local_step(tokens, cot, rel_index, weights)
+        result, pairs, smalls, extras = local_step(tokens, cot, rel_index, weights)
         table_len, n_heads = weights[5].shape
-        *grads, small, result = reduce_all(pairs, smalls, g_pos, rel_index, result, n_heads, table_len)
-        large, smalls, g_table = finish(grads + [result], small, [x.shape for x in smalls], n_heads, table_len)
-        g_w2, g_w1, g_wr, g_wq, g_wp, result = large
-        g_nm, g_na, g_nb, g_bq, g_bp, g_b1, g_b2 = smalls
+        *grads, small, result, g_tok = reduce_all(pairs, smalls, extras, result, tokens, n_heads, table_len)
+        small_shapes = [x.shape for x in smalls] + [weights[0].shape]
+        large, smalls, g_table = finish(grads + [result, g_tok], small, small_shapes, n_heads, table_len)
+        g_w2, g_w1, g_wq, g_wp, g_wr, result, g_tok = large
+        g_na, g_nb, g_bq, g_bp, g_b1, g_b2, g_nm = smalls
         return (result.reshape(grad_out.shape), g_tok, g_nm, g_wr, g_na, g_wq, g_bq.reshape(-1), g_table, g_wp, g_bp.reshape(-1), g_nb,
                 g_w1, g_b1.reshape(-1), g_w2, g_b2.reshape(-1))
 

time: 245 us -> 238 us (0.971)
  Pallas kernels: 236 us -> 230 us
    pallas_call x4, Pallas kernels: 79.1 us -> 72 us  [call(): pl.pallas_call(kernel, grid=grid, in_specs=in_specs, out_specs=out_specs,...]
  transfers between devices with their start and end apart: 1 -> 1, of which waited for: 0 -> 0; matrix products, arithmetic and copies ran while one was open for 0% -> 0% of each run, Pallas kernels for 12% -> 13%
where the time goes in v5:
time: 238 us
  Pallas kernels  230 us (97%)
  starting transfers between devices  4.28 us (2%)
    pallas_call x1, Pallas kernels, reduce_all(): pl.pallas_call(functools.partial(reduce_kernel, n=n, n_small=len(smalls),...  144 us
    pallas_call x4, Pallas kernels, call(): pl.pallas_call(kernel, grid=grid, in_specs=in_specs, out_specs=out_specs,...  72 us
    pallas_call x1, Pallas kernels, finish(): pl.pallas_call(functools.partial(finish_kernel, n=n, cuts=cuts), in_specs...  14.6 us
  transfers between devices with their start and end apart: 1, of which 0 were waited for; matrix products, arithmetic and copies ran while one was open for 0% of the time, Pallas kernels for 13%

profile of v5, /device:TPU:0, one launch (start us, length us, event | category | flops | bytes accessed | tf_op | source)
XLA Modules:
  0.0 238.1 jit_solution(11437727647879945689)
XLA Ops:
  0.6 0.0 copy-start.1
  0.7 4.3 %all-to-all-start = ((bf16[1,48,24,512]{3,2,0,1:T(8,128)(2,1)}), bf16[1,48,24,512]{3,2,0,1:T(8,128)(2,1)S(1)}, u32[]{:S(2)}, u32[]{:S(2)}) async-start(bf16[1,48,24,512]{3,2,0,1:T(8,128)(2,1)} %bitcast.28), calls=%async_computation | async-start | bytes 2359296 | tf_op jit(solution)/shard_map/all_to_all | solution.py:610
  4.9 0.0 copy-done.1
  4.9 0.6 pad_convert_fusion.table_ref
  5.6 10.8 %pos.1.pos_ref = f32[2,144,1152]{2,1,0:T(8,128)} custom-call(f32[16,640]{1,0:T(8,128)} %pad_convert_fusion.table_ref, s32[144,144]{1,0:T(8,128)} %refs_20_.1), custom_call_target="tpu_custom_call" | custom-call | flops 10000000 | bytes 1451008 | tf_op jit(solution)/shard_map/pos/pallas_call | solution.py:251
  16.4 19.4 %fwd.1 = (bf16[4,288,1024]{2,1,0:T(8,128)(2,1)}, bf16[4,288,512]{2,1,0:T(8,128)(2,1)}, bf16[4,288,1536]{2,1,0:T(8,128)(2,1)}, bf16[4,288,512]{2,1,0:T(8,128)(2,1...) custom-call(bf16[4,24,48,256]{3,2,1,0:T(8,128)(2,1)} %tok_ref.1, ...), custom_call_target="tpu_custom_call" | custom-call | flops 8000000000 | bytes 16648192 | tf_op jit(solution)/shard_map/fwd/pallas_call | solution.py:251
  35.8 0.0 all-to-all-done
  35.8 0.0 copy-start
  35.8 1.0 copy-done
  36.9 20.5 %mlp.1 = (bf16[4,288,512]{2,1,0:T(8,128)(2,1)}, f32[4,288,512]{2,1,0:T(8,128)}, bf16[4,288,2048]{2,1,0:T(8,128)(2,1)}, bf16[4,288,2048]{2,1,0:T(8,128)(2,1)}, bf...) custom-call(bf16[4,288,512]{2,1,0:T(8,128)(2,1)} %get-tuple-element., ...), custom_call_target="tpu_custom_call" | custom-call | flops 12000000000 | bytes 22076416 | tf_op jit(solution)/shard_map/mlp/pallas_call | solution.py:251
  57.3 21.2 %bwd.1 = (bf16[4,288,512]{2,1,0:T(8,128)(2,1)}, bf16[4,288,512]{2,1,0:T(8,128)(2,1)}, bf16[4,288,1536]{2,1,0:T(8,128)(2,1)}, bf16[4,288,512]{2,1,0:T(8,128)(2,1)...) custom-call(f32[4,288,512]{2,1,0:T(8,128)} %get-tuple-element.66.dh1_ref, ...), custom_call_target="tpu_custom_call" | custom-call | flops 12000000000 | bytes 18995200 | tf_op jit(solution)/shard_map/bwd/pallas_call | solution.py:251
  78.6 143.6 %reduce.2 = (f32[2048,512]{1,0:T(8,128)}, f32[512,2048]{1,0:T(8,128)}, f32[512,1536]{1,0:T(8,128)}, f32[512,512]{1,0:T(8,128)}, f32[1024,512]{1,0:T(8,128)}, /*i...) custom-call(bf16[1152,2048]{1,0:T(8,128)(2,1)} %bitcast.18, ...), custom_call_target="tpu_custom_call" | custom-call | tf_op jit(solution)/shard_map/reduce/pallas_call | solution.py:557
  222.2 14.6 %finish.1 = (f32[2048,512]{1,0:T(8,128)}, f32[512,2048]{1,0:T(8,128)}, f32[512,1536]{1,0:T(8,128)}, f32[512,512]{1,0:T(8,128)}, f32[1024,512]{1,0:T(8,128)}, /*i...) custom-call(f32[2048,512]{1,0:T(8,128)} %get-tuple-element.84.refs_0, ...), custom_call_target="tpu_custom_call" | custom-call | tf_op jit(solution)/shard_map/finish/pallas_call | solution.py:601
  236.8 1.3 reduce.1
Async XLA Ops:
  0.6 4.3 %copy-start.1 = (bf16[529,16]{0,1:T(8,128)(2,1)S(1)}, bf16[529,16]{0,1:T(8,128)(2,1)}, u32[]{:S(2)}) copy-start(bf16[529,16]{0,1:T(8,128)(2,1)} %param.26) | copy-start | bytes 50788
  0.7 35.2 %all-to-all-start = ((bf16[1,48,24,512]{3,2,0,1:T(8,128)(2,1)}), bf16[1,48,24,512]{3,2,0,1:T(8,128)(2,1)S(1)}, u32[]{:S(2)}, u32[]{:S(2)}) async-start(bf16[1,48,24,512]{3,2,0,1:T(8,128)(2,1)} %bitcast.28), calls=%async_computation | async-start | bytes 2359296 | tf_op jit(solution)/shard_map/all_to_all | solution.py:610
  35.8 1.0 copy-start
